TPU v7x, 256 devices: a whole 4x4x8 slice. The times are simulated.
256 devices in a mesh: ulysses: 32 (over z, x), blk: 8 (over y, core).
Axes of the slice: x: 4, y: 4, z: 8, core: 2. Of those that a mesh axis runs over, the one named last changes fastest.
Arguments:
- queries: bfloat16 [16384, 4096], P(('ulysses', 'blk')), may hold values from -6 to 6
- key_rows: bfloat16 [16384, 1024], P(('ulysses', 'blk')), may hold values from -6 to 6
- value_rows: bfloat16 [16384, 1024], P(('ulysses', 'blk')), may hold values from -6 to 6
Outputs:
- attended: bfloat16 [16384, 4096], P(('ulysses', 'blk'))
All inputs are finite; a program needn't handle non-finite values.
Results may differ from a plain program's by a relative error of at most 0.006.
Values may be sent and summed in bfloat16 or wider, within the bound.
No kernel may reach another device: no remote copies, remote signals or barrier semaphores. Data moves between devices by JAX's collectives and lax.ppermute only.
A program may use at most 64 MiB of HBM per device.

v0:
```python
import math

import jax
import jax.numpy as jnp
from jax import lax
from jax.sharding import PartitionSpec as P

Q_HEADS = 32
KV_HEADS = 8
HEAD_DIM = 128


masked_score = -1e30


def cut_along(x, dim, length):
    before, after = (x.shape[:dim], x.shape[dim + 1 :])
    return jnp.moveaxis(x.reshape(*before, length, -1, *after), dim, 0)


def cut_rows(length, count):
    turn = length // count
    if turn >= 8:
        turn -= turn % 8
    return [turn * k for k in range(1, count)]


def in_order(parts, dim):
    parts = jnp.moveaxis(parts, 0, dim)
    shape = parts.shape
    return parts.reshape(*shape[:dim], shape[dim] * shape[dim + 1], *shape[dim + 2 :])


def several_exchanges(x, axis, pieces, split_dim, concat_dim):
    parts = cut_along(x, split_dim, lax.axis_size(axis))
    split_at = max(range(1, max(2, parts.ndim - 1)), key=lambda d: parts.shape[d])
    finished = []
    for share in jnp.split(parts, cut_rows(parts.shape[split_at], pieces), axis=split_at):
        if share.size:
            finished.append(lax.all_to_all(share, axis, split_axis=0, concat_axis=0, tiled=True))
    return in_order(jnp.concatenate(finished, axis=split_at), concat_dim)


def from_behind(value, axis, steps):
    count = lax.axis_size(axis)
    pairs = [(source, (source + steps) % count) for source in range(count)]
    return lax.ppermute(value, axis, pairs)


def positions(span_rows, tok_rows, block_count, source):
    index = jnp.arange(span_rows, dtype=jnp.int32)
    return (index // tok_rows * block_count + source) * tok_rows + index % tok_rows


def attend(state, queries_h, block, query_where, key_where, tile_rows):
    span_rows = queries_h.shape[2]
    tile_count = span_rows // tile_rows
    scale = 1.0 / math.sqrt(queries_h.shape[3])

    def per_query(query_tile, carry):
        maxima, totals, sums = carry
        first = query_tile * tile_rows
        q_part = lax.dynamic_slice_in_dim(queries_h, first, tile_rows, 2)
        q_where = lax.dynamic_slice_in_dim(query_where, first, tile_rows, 0)
        inner = (
            lax.dynamic_slice_in_dim(maxima, first, tile_rows, 2),
            lax.dynamic_slice_in_dim(totals, first, tile_rows, 2),
            lax.dynamic_slice_in_dim(sums, first, tile_rows, 2),
        )

        def per_key(key_tile, running):
            top, total, summed = running
            start = key_tile * tile_rows
            kv_part = lax.dynamic_slice_in_dim(block, start, tile_rows, 0)
            k_where = lax.dynamic_slice_in_dim(key_where, start, tile_rows, 0)
            scores = (
                jnp.einsum(
                    "cgtd,scd->cgts",
                    q_part,
                    kv_part[:, :, 0, :],
                    preferred_element_type=jnp.float32,
                )
                * scale
            )
            allowed = k_where[None, :] <= q_where[:, None]
            scores = jnp.where(allowed, scores, masked_score)
            new_top = jnp.maximum(top, jnp.max(scores, axis=-1))
            factor = jnp.exp(top - new_top)
            weights = jnp.where(allowed, jnp.exp(scores - new_top[..., None]), 0.0)
            total = total * factor + jnp.sum(weights, axis=-1)
            summed = summed * factor[..., None] + jnp.einsum(
                "cgts,scd->cgtd",
                weights.astype(jnp.bfloat16),
                kv_part[:, :, 1, :],
                preferred_element_type=jnp.float32,
            )
            return (new_top, total, summed)

        top, total, summed = lax.fori_loop(0, query_tile + 1, per_key, inner)
        maxima = lax.dynamic_update_slice_in_dim(maxima, top, first, 2)
        totals = lax.dynamic_update_slice_in_dim(totals, total, first, 2)
        sums = lax.dynamic_update_slice_in_dim(sums, summed, first, 2)
        return (maxima, totals, sums)

    return lax.fori_loop(0, tile_count, per_query, state)


def per_device(queries, key_rows, value_rows):
    group_size = lax.axis_size("ulysses")
    block_count = lax.axis_size("blk")
    my_block = lax.axis_index("blk")
    tok_rows = queries.shape[0]
    heads_here = Q_HEADS // group_size
    repeat = max(1, group_size // KV_HEADS)
    kv_here = max(1, KV_HEADS // group_size)
    per_kv = heads_here // kv_here
    keys_split = key_rows.reshape(tok_rows, KV_HEADS, 1, HEAD_DIM)
    values_split = value_rows.reshape(tok_rows, KV_HEADS, 1, HEAD_DIM)
    paired = jnp.concatenate((keys_split, values_split), axis=2)
    paired = jnp.broadcast_to(paired[:, :, None], (tok_rows, KV_HEADS, repeat, 2, HEAD_DIM))
    paired = paired.reshape(tok_rows, KV_HEADS * repeat * 2 * HEAD_DIM)
    q_heads, kv_heads = (
        several_exchanges(queries, "ulysses", 2, 1, 0),
        several_exchanges(paired, "ulysses", 2, 1, 0),
    )
    span_rows = q_heads.shape[0]
    queries_h = q_heads.reshape(span_rows, kv_here, per_kv, HEAD_DIM).transpose(1, 2, 0, 3)
    own_block = kv_heads.reshape(span_rows, kv_here, 2, HEAD_DIM)
    tile_rows = min(512, span_rows)
    query_where = positions(span_rows, tok_rows, block_count, my_block)
    state = (
        jnp.full((kv_here, per_kv, span_rows), masked_score, jnp.float32),
        jnp.zeros((kv_here, per_kv, span_rows), jnp.float32),
        jnp.zeros((kv_here, per_kv, span_rows, HEAD_DIM), jnp.float32),
    )
    current = own_block
    for turn in range(block_count):
        if turn + 1 < block_count:
            following = from_behind(current, "blk", 1)
        key_where = positions(span_rows, tok_rows, block_count, (my_block - turn) % block_count)
        state = attend(state, queries_h, current, query_where, key_where, tile_rows)
        if turn + 1 < block_count:
            current = following
    maxima, totals, sums = state
    mixed = (sums / totals[..., None]).astype(jnp.bfloat16)
    mixed = mixed.transpose(2, 0, 1, 3).reshape(span_rows, heads_here * HEAD_DIM)
    return lax.all_to_all(mixed, "ulysses", split_axis=0, concat_axis=1, tiled=True)


def solution(mesh):
    in_specs = (
        P(("ulysses", "blk"), None),
        P(("ulysses", "blk"), None),
        P(("ulysses", "blk"), None),
    )
    out_specs = P(("ulysses", "blk"), None)
    return jax.shard_map(
        per_device, mesh=mesh, in_specs=in_specs, out_specs=out_specs, check_vma=False
    )
```

profile of v0, /device:TPU:1, one launch (start us, length us, event | category | flops | bytes accessed | tf_op | source)
XLA Modules:
  0.0 655.9 jit_solution(17591677336243681494)
XLA Ops:
  2.0 22.9 %all_to_all.39 = bf16[32,32,128]{2,1,0:T(8,128)(2,1)S(1)} all-to-all(bf16[32,32,128]{2,1,0:T(8,128)(2,1)S(1)} %get-tuple-element.2245), channel_id=1, replica_groups=mesh['ulysses'=32,'blk'=8] {'ulysses'}, dimensions={0} | all-to-all | bytes 524288 | tf_op jit(solution)/shard_map/all_to_all | solution.py:40
  24.9 4.8 all-to-all-start.1
  32.7 7.5 %all-to-all-done.1 = bf16[32,32,128]{2,1,0:T(8,128)(2,1)} async-done(((bf16[32,32,128]{2,1,0:T(8,128)(2,1)}), bf16[32,32,128]{2,1,0:T(8,128)(2,1)}, u32[]{:S(2)}, u32[]{:S(2)}) %all-to-all-start.1) | async-done | bytes 262176 | tf_op jit(solution)/shard_map/all_to_all | solution.py:40
  40.1 17.3 %all_to_all.40 = bf16[32,32,256]{2,1,0:T(8,128)(2,1)S(1)} all-to-all(bf16[32,32,256]{2,1,0:T(8,128)(2,1)S(1)} %get-tuple-element.2243), channel_id=1, replica_groups=mesh['ulysses'=32,'blk'=8] {'ulysses'}, dimensions={0} | all-to-all | bytes 1048576 | tf_op jit(solution)/shard_map/all_to_all | solution.py:40
  57.5 6.1 all-to-all-start.3
  65.3 11.1 %all-to-all-done.3 = bf16[32,32,256]{2,1,0:T(8,128)(2,1)S(1)} async-done(((bf16[32,32,256]{2,1,0:T(8,128)(2,1)}), bf16[32,32,256]{2,1,0:T(8,128)(2,1)S(1)}, u32[]{:S(2)}, u32[]{:S(2)}) %all-to-all-start.3) | async-done | bytes 524320 | tf_op jit(solution)/shard_map/all_to_all | solution.py:40
  77.7 2.3 copy.33
  80.0 7.2 %collective-permute-start = (bf16[2048,1,2,128]{3,2,0,1:T(2,128)(2,1)}, bf16[2048,1,2,128]{3,2,0,1:T(2,128)(2,1)}, u32[]{:S(2)}, u32[]{:S(2)}) collective-permute-start(bf16[2048,1,2,128]{3,2,0,1:T(2,128)(2,1)} %reshape_reshape.7), channel_id=1, source_target_pairs={{0,1},{1,2},{2,3},{3,4},{4,5},{5,6},{6,7},{7,0},{8,9},{9,10},{10,1... | collective-permute-start | bytes 3145736 | tf_op jit(solution)/shard_map/ppermute | solution.py:47
  88.5 65.7 %while.425 = (s32[]{:T(128)}, f32[1,1,2048]{2,1,0:T(1,128)}, f32[1,1,2048]{2,1,0:T(1,128)}, f32[1,1,2048,128]{3,2,1,0:T(8,128)S(1)}, bf16[1,1,2048,128]{3,2,1,0:...) while((s32[]{:T(128)}, f32[1,1,2048]{2,1,0:T(1,128)}, ...), condition=%wide.region_5.6_spmd.clone, body=%wide.region_0.5_spmd.clone.sunk | while | flops 137528320 | bytes 5452338 | solution.py:105
  91.8 5.0 while.440
  100.7 10.0 %while.440 = (s32[]{:T(128)}, f32[1,1,512]{2,1,0:T(1,128)S(1)}, f32[1,1,512]{2,1,0:T(1,128)S(1)}, f32[1,1,512,128]{3,2,1,0:T(8,128)S(1)}, s32[]{:T(128)}, /*inde...) while((s32[]{:T(128)}, f32[1,1,512]{2,1,0:T(1,128)S(1)}, ...), condition=%wide.region_4.4_spmd, body=%wide.region_1.3_spmd.sunk | while | flops 137495552 | bytes 4112591 | solution.py:99
  104.2 1.5 fusion.318
  114.7 14.9 %while.440 = (s32[]{:T(128)}, f32[1,1,512]{2,1,0:T(1,128)S(1)}, f32[1,1,512]{2,1,0:T(1,128)S(1)}, f32[1,1,512,128]{3,2,1,0:T(8,128)S(1)}, s32[]{:T(128)}, /*inde...) while((s32[]{:T(128)}, f32[1,1,512]{2,1,0:T(1,128)S(1)}, ...), condition=%wide.region_4.4_spmd, body=%wide.region_1.3_spmd.sunk | while | flops 137495552 | bytes 4112591 | solution.py:99
  133.6 19.9 %while.440 = (s32[]{:T(128)}, f32[1,1,512]{2,1,0:T(1,128)S(1)}, f32[1,1,512]{2,1,0:T(1,128)S(1)}, f32[1,1,512,128]{3,2,1,0:T(8,128)S(1)}, s32[]{:T(128)}, /*inde...) while((s32[]{:T(128)}, f32[1,1,512]{2,1,0:T(1,128)S(1)}, ...), condition=%wide.region_4.4_spmd, body=%wide.region_1.3_spmd.sunk | while | flops 137495552 | bytes 4112591 | solution.py:99
  154.1 2.3 copy.34
  156.5 65.7 %while.427 = (s32[]{:T(128)}, f32[1,1,2048]{2,1,0:T(1,128)}, f32[1,1,2048]{2,1,0:T(1,128)}, f32[1,1,2048,128]{3,2,1,0:T(8,128)S(1)}, bf16[1,1,2048,128]{3,2,1,0:...) while((s32[]{:T(128)}, f32[1,1,2048]{2,1,0:T(1,128)}, ...), condition=%wide.region_11.12_spmd.clone, body=%wide.region_6.11_spmd.clone.sunk | while | flops 137528320 | bytes 5452338 | solution.py:105
  159.8 5.0 while.441
  168.8 10.0 %while.441 = (s32[]{:T(128)}, f32[1,1,512]{2,1,0:T(1,128)S(1)}, f32[1,1,512]{2,1,0:T(1,128)S(1)}, f32[1,1,512,128]{3,2,1,0:T(8,128)S(1)}, s32[]{:T(128)}, /*inde...) while((s32[]{:T(128)}, f32[1,1,512]{2,1,0:T(1,128)S(1)}, ...), condition=%wide.region_10.10_spmd, body=%wide.region_7.9_spmd.sunk | while | flops 137495552 | bytes 4112591 | solution.py:99
  172.2 1.5 fusion.314
  182.7 14.9 %while.441 = (s32[]{:T(128)}, f32[1,1,512]{2,1,0:T(1,128)S(1)}, f32[1,1,512]{2,1,0:T(1,128)S(1)}, f32[1,1,512,128]{3,2,1,0:T(8,128)S(1)}, s32[]{:T(128)}, /*inde...) while((s32[]{:T(128)}, f32[1,1,512]{2,1,0:T(1,128)S(1)}, ...), condition=%wide.region_10.10_spmd, body=%wide.region_7.9_spmd.sunk | while | flops 137495552 | bytes 4112591 | solution.py:99
  201.6 19.9 %while.441 = (s32[]{:T(128)}, f32[1,1,512]{2,1,0:T(1,128)S(1)}, f32[1,1,512]{2,1,0:T(1,128)S(1)}, f32[1,1,512,128]{3,2,1,0:T(8,128)S(1)}, s32[]{:T(128)}, /*inde...) while((s32[]{:T(128)}, f32[1,1,512]{2,1,0:T(1,128)S(1)}, ...), condition=%wide.region_10.10_spmd, body=%wide.region_7.9_spmd.sunk | while | flops 137495552 | bytes 4112591 | solution.py:99
  205.1 1.5 fusion.314
  220.0 1.5 fusion.314
  222.2 2.3 copy.35
  224.5 1.7 collective-permute-start.2
  226.2 65.7 %while.429 = (s32[]{:T(128)}, f32[1,1,2048]{2,1,0:T(1,128)}, f32[1,1,2048]{2,1,0:T(1,128)}, f32[1,1,2048,128]{3,2,1,0:T(8,128)S(1)}, bf16[1,1,2048,128]{3,2,1,0:...) while((s32[]{:T(128)}, f32[1,1,2048]{2,1,0:T(1,128)}, ...), condition=%wide.region_17.18_spmd.clone, body=%wide.region_12.17_spmd.clone.sunk | while | flops 137528320 | bytes 5452338 | solution.py:105
  229.5 5.0 while.442
  238.4 10.0 %while.442 = (s32[]{:T(128)}, f32[1,1,512]{2,1,0:T(1,128)S(1)}, f32[1,1,512]{2,1,0:T(1,128)S(1)}, f32[1,1,512,128]{3,2,1,0:T(8,128)S(1)}, s32[]{:T(128)}, /*inde...) while((s32[]{:T(128)}, f32[1,1,512]{2,1,0:T(1,128)S(1)}, ...), condition=%wide.region_16.16_spmd, body=%wide.region_13.15_spmd.sunk | while | flops 137495552 | bytes 4112591 | solution.py:99
  252.4 14.9 %while.442 = (s32[]{:T(128)}, f32[1,1,512]{2,1,0:T(1,128)S(1)}, f32[1,1,512]{2,1,0:T(1,128)S(1)}, f32[1,1,512,128]{3,2,1,0:T(8,128)S(1)}, s32[]{:T(128)}, /*inde...) while((s32[]{:T(128)}, f32[1,1,512]{2,1,0:T(1,128)S(1)}, ...), condition=%wide.region_16.16_spmd, body=%wide.region_13.15_spmd.sunk | while | flops 137495552 | bytes 4112591 | solution.py:99
  271.3 19.9 %while.442 = (s32[]{:T(128)}, f32[1,1,512]{2,1,0:T(1,128)S(1)}, f32[1,1,512]{2,1,0:T(1,128)S(1)}, f32[1,1,512,128]{3,2,1,0:T(8,128)S(1)}, s32[]{:T(128)}, /*inde...) while((s32[]{:T(128)}, f32[1,1,512]{2,1,0:T(1,128)S(1)}, ...), condition=%wide.region_16.16_spmd, body=%wide.region_13.15_spmd.sunk | while | flops 137495552 | bytes 4112591 | solution.py:99
  279.7 1.5 fusion.310
  291.9 2.3 copy.36
  294.2 65.7 %while.431 = (s32[]{:T(128)}, f32[1,1,2048]{2,1,0:T(1,128)}, f32[1,1,2048]{2,1,0:T(1,128)}, f32[1,1,2048,128]{3,2,1,0:T(8,128)S(1)}, bf16[1,1,2048,128]{3,2,1,0:...) while((s32[]{:T(128)}, f32[1,1,2048]{2,1,0:T(1,128)}, ...), condition=%wide.region_23.24_spmd.clone, body=%wide.region_18.23_spmd.clone.sunk | while | flops 137528320 | bytes 5452338 | solution.py:105
  297.6 5.0 while.443
  306.5 10.0 %while.443 = (s32[]{:T(128)}, f32[1,1,512]{2,1,0:T(1,128)S(1)}, f32[1,1,512]{2,1,0:T(1,128)S(1)}, f32[1,1,512,128]{3,2,1,0:T(8,128)S(1)}, s32[]{:T(128)}, /*inde...) while((s32[]{:T(128)}, f32[1,1,512]{2,1,0:T(1,128)S(1)}, ...), condition=%wide.region_22.22_spmd, body=%wide.region_19.21_spmd.sunk | while | flops 137495552 | bytes 4112591 | solution.py:99
  320.4 14.9 %while.443 = (s32[]{:T(128)}, f32[1,1,512]{2,1,0:T(1,128)S(1)}, f32[1,1,512]{2,1,0:T(1,128)S(1)}, f32[1,1,512,128]{3,2,1,0:T(8,128)S(1)}, s32[]{:T(128)}, /*inde...) while((s32[]{:T(128)}, f32[1,1,512]{2,1,0:T(1,128)S(1)}, ...), condition=%wide.region_22.22_spmd, body=%wide.region_19.21_spmd.sunk | while | flops 137495552 | bytes 4112591 | solution.py:99
  339.3 19.9 %while.443 = (s32[]{:T(128)}, f32[1,1,512]{2,1,0:T(1,128)S(1)}, f32[1,1,512]{2,1,0:T(1,128)S(1)}, f32[1,1,512,128]{3,2,1,0:T(8,128)S(1)}, s32[]{:T(128)}, /*inde...) while((s32[]{:T(128)}, f32[1,1,512]{2,1,0:T(1,128)S(1)}, ...), condition=%wide.region_22.22_spmd, body=%wide.region_19.21_spmd.sunk | while | flops 137495552 | bytes 4112591 | solution.py:99
  342.8 1.5 fusion.306
  359.9 2.3 copy.37
  363.6 65.7 %while.433 = (s32[]{:T(128)}, f32[1,1,2048]{2,1,0:T(1,128)}, f32[1,1,2048]{2,1,0:T(1,128)}, f32[1,1,2048,128]{3,2,1,0:T(8,128)S(1)}, bf16[1,1,2048,128]{3,2,1,0:...) while((s32[]{:T(128)}, f32[1,1,2048]{2,1,0:T(1,128)}, ...), condition=%wide.region_29.30_spmd.clone, body=%wide.region_24.29_spmd.clone.sunk | while | flops 137528320 | bytes 5452338 | solution.py:105
  366.9 5.0 while.444
  370.4 1.5 fusion.302
  375.9 10.0 %while.444 = (s32[]{:T(128)}, f32[1,1,512]{2,1,0:T(1,128)S(1)}, f32[1,1,512]{2,1,0:T(1,128)S(1)}, f32[1,1,512,128]{3,2,1,0:T(8,128)S(1)}, s32[]{:T(128)}, /*inde...) while((s32[]{:T(128)}, f32[1,1,512]{2,1,0:T(1,128)S(1)}, ...), condition=%wide.region_28.28_spmd, body=%wide.region_25.27_spmd.sunk | while | flops 137495552 | bytes 4112591 | solution.py:99
  389.8 14.9 %while.444 = (s32[]{:T(128)}, f32[1,1,512]{2,1,0:T(1,128)S(1)}, f32[1,1,512]{2,1,0:T(1,128)S(1)}, f32[1,1,512,128]{3,2,1,0:T(8,128)S(1)}, s32[]{:T(128)}, /*inde...) while((s32[]{:T(128)}, f32[1,1,512]{2,1,0:T(1,128)S(1)}, ...), condition=%wide.region_28.28_spmd, body=%wide.region_25.27_spmd.sunk | while | flops 137495552 | bytes 4112591 | solution.py:99
  408.7 19.9 %while.444 = (s32[]{:T(128)}, f32[1,1,512]{2,1,0:T(1,128)S(1)}, f32[1,1,512]{2,1,0:T(1,128)S(1)}, f32[1,1,512,128]{3,2,1,0:T(8,128)S(1)}, s32[]{:T(128)}, /*inde...) while((s32[]{:T(128)}, f32[1,1,512]{2,1,0:T(1,128)S(1)}, ...), condition=%wide.region_28.28_spmd, body=%wide.region_25.27_spmd.sunk | while | flops 137495552 | bytes 4112591 | solution.py:99
  429.3 2.3 copy.38
  431.7 65.7 %while.435 = (s32[]{:T(128)}, f32[1,1,2048]{2,1,0:T(1,128)}, f32[1,1,2048]{2,1,0:T(1,128)}, f32[1,1,2048,128]{3,2,1,0:T(8,128)S(1)}, bf16[1,1,2048,128]{3,2,1,0:...) while((s32[]{:T(128)}, f32[1,1,2048]{2,1,0:T(1,128)}, ...), condition=%wide.region_35.36_spmd.clone, body=%wide.region_30.35_spmd.clone.sunk | while | flops 137528320 | bytes 5452338 | solution.py:105
  435.0 5.0 while.445
  443.9 10.0 %while.445 = (s32[]{:T(128)}, f32[1,1,512]{2,1,0:T(1,128)S(1)}, f32[1,1,512]{2,1,0:T(1,128)S(1)}, f32[1,1,512,128]{3,2,1,0:T(8,128)S(1)}, s32[]{:T(128)}, /*inde...) while((s32[]{:T(128)}, f32[1,1,512]{2,1,0:T(1,128)S(1)}, ...), condition=%wide.region_34.34_spmd, body=%wide.region_31.33_spmd.sunk | while | flops 137495552 | bytes 4112591 | solution.py:99
  457.8 14.9 %while.445 = (s32[]{:T(128)}, f32[1,1,512]{2,1,0:T(1,128)S(1)}, f32[1,1,512]{2,1,0:T(1,128)S(1)}, f32[1,1,512,128]{3,2,1,0:T(8,128)S(1)}, s32[]{:T(128)}, /*inde...) while((s32[]{:T(128)}, f32[1,1,512]{2,1,0:T(1,128)S(1)}, ...), condition=%wide.region_34.34_spmd, body=%wide.region_31.33_spmd.sunk | while | flops 137495552 | bytes 4112591 | solution.py:99
  476.7 19.9 %while.445 = (s32[]{:T(128)}, f32[1,1,512]{2,1,0:T(1,128)S(1)}, f32[1,1,512]{2,1,0:T(1,128)S(1)}, f32[1,1,512,128]{3,2,1,0:T(8,128)S(1)}, s32[]{:T(128)}, /*inde...) while((s32[]{:T(128)}, f32[1,1,512]{2,1,0:T(1,128)S(1)}, ...), condition=%wide.region_34.34_spmd, body=%wide.region_31.33_spmd.sunk | while | flops 137495552 | bytes 4112591 | solution.py:99
  497.3 2.3 copy.39
  500.0 65.7 %while.437 = (s32[]{:T(128)}, f32[1,1,2048]{2,1,0:T(1,128)}, f32[1,1,2048]{2,1,0:T(1,128)}, f32[1,1,2048,128]{3,2,1,0:T(8,128)S(1)}, bf16[1,1,2048,128]{3,2,1,0:...) while((s32[]{:T(128)}, f32[1,1,2048]{2,1,0:T(1,128)}, ...), condition=%wide.region_41.42_spmd.clone, body=%wide.region_36.41_spmd.clone.sunk | while | flops 137528320 | bytes 5452338 | solution.py:105
  503.3 5.0 while.446
  512.2 10.0 %while.446 = (s32[]{:T(128)}, f32[1,1,512]{2,1,0:T(1,128)S(1)}, f32[1,1,512]{2,1,0:T(1,128)S(1)}, f32[1,1,512,128]{3,2,1,0:T(8,128)S(1)}, s32[]{:T(128)}, /*inde...) while((s32[]{:T(128)}, f32[1,1,512]{2,1,0:T(1,128)S(1)}, ...), condition=%wide.region_40.40_spmd, body=%wide.region_37.39_spmd.sunk | while | flops 137495552 | bytes 4112591 | solution.py:99
  526.2 14.9 %while.446 = (s32[]{:T(128)}, f32[1,1,512]{2,1,0:T(1,128)S(1)}, f32[1,1,512]{2,1,0:T(1,128)S(1)}, f32[1,1,512,128]{3,2,1,0:T(8,128)S(1)}, s32[]{:T(128)}, /*inde...) while((s32[]{:T(128)}, f32[1,1,512]{2,1,0:T(1,128)S(1)}, ...), condition=%wide.region_40.40_spmd, body=%wide.region_37.39_spmd.sunk | while | flops 137495552 | bytes 4112591 | solution.py:99
  545.1 19.9 %while.446 = (s32[]{:T(128)}, f32[1,1,512]{2,1,0:T(1,128)S(1)}, f32[1,1,512]{2,1,0:T(1,128)S(1)}, f32[1,1,512,128]{3,2,1,0:T(8,128)S(1)}, s32[]{:T(128)}, /*inde...) while((s32[]{:T(128)}, f32[1,1,512]{2,1,0:T(1,128)S(1)}, ...), condition=%wide.region_40.40_spmd, body=%wide.region_37.39_spmd.sunk | while | flops 137495552 | bytes 4112591 | solution.py:99
  565.6 2.4 copy.40
  568.0 65.4 %while.439 = (s32[]{:T(128)}, f32[1,1,2048]{2,1,0:T(1,128)}, f32[1,1,2048]{2,1,0:T(1,128)}, f32[1,1,2048,128]{3,2,1,0:T(8,128)S(1)}, bf16[1,1,2048,128]{3,2,1,0:...) while((s32[]{:T(128)}, f32[1,1,2048]{2,1,0:T(1,128)}, ...), condition=%wide.region_47.48_spmd.clone, body=%wide.region_42.47_spmd.clone.sunk | while | flops 137528320 | bytes 5452338 | solution.py:105
  571.3 4.9 while.447
  580.2 9.9 %while.447 = (s32[]{:T(128)}, f32[1,1,512]{2,1,0:T(1,128)S(1)}, f32[1,1,512]{2,1,0:T(1,128)S(1)}, f32[1,1,512,128]{3,2,1,0:T(8,128)S(1)}, s32[]{:T(128)}, /*inde...) while((s32[]{:T(128)}, f32[1,1,512]{2,1,0:T(1,128)S(1)}, ...), condition=%wide.region_46.46_spmd, body=%wide.region_43.45_spmd.sunk | while | flops 137495552 | bytes 4112591 | solution.py:99
  594.1 14.9 %while.447 = (s32[]{:T(128)}, f32[1,1,512]{2,1,0:T(1,128)S(1)}, f32[1,1,512]{2,1,0:T(1,128)S(1)}, f32[1,1,512,128]{3,2,1,0:T(8,128)S(1)}, s32[]{:T(128)}, /*inde...) while((s32[]{:T(128)}, f32[1,1,512]{2,1,0:T(1,128)S(1)}, ...), condition=%wide.region_46.46_spmd, body=%wide.region_43.45_spmd.sunk | while | flops 137495552 | bytes 4112591 | solution.py:99
  613.0 19.9 %while.447 = (s32[]{:T(128)}, f32[1,1,512]{2,1,0:T(1,128)S(1)}, f32[1,1,512]{2,1,0:T(1,128)S(1)}, f32[1,1,512,128]{3,2,1,0:T(8,128)S(1)}, s32[]{:T(128)}, /*inde...) while((s32[]{:T(128)}, f32[1,1,512]{2,1,0:T(1,128)S(1)}, ...), condition=%wide.region_46.46_spmd, body=%wide.region_43.45_spmd.sunk | while | flops 137495552 | bytes 4112591 | solution.py:99
  634.5 20.6 %all_to_all.41 = bf16[32,64,128]{2,1,0:T(8,128)(2,1)S(1)} all-to-all(bf16[32,64,128]{2,1,0:T(8,128)(2,1)S(1)} %bitcast.381), channel_id=1, replica_groups=mesh['ulysses'=32,'blk'=8] {'ulysses'}, dimensions={0} | all-to-all | bytes 1048576 | tf_op jit(solution)/shard_map/all_to_all | solution.py:147
  (845 shorter events, 523.1 us)
Async XLA Ops:
  0.0 1.0 copy-start
  1.2 28.6 %copy-start.1 = (bf16[64,1024]{1,0:T(8,128)(2,1)S(1)}, bf16[64,1024]{1,0:T(8,128)(2,1)}, u32[]{:S(2)}) copy-start(bf16[64,1024]{1,0:T(8,128)(2,1)} %param.36) | copy-start | bytes 393220
  1.2 28.6 %copy-start.2 = (bf16[64,1024]{1,0:T(8,128)(2,1)S(1)}, bf16[64,1024]{1,0:T(8,128)(2,1)}, u32[]{:S(2)}) copy-start(bf16[64,1024]{1,0:T(8,128)(2,1)} %param.37) | copy-start | bytes 393220
  24.9 15.2 %all-to-all-start.1 = ((bf16[32,32,128]{2,1,0:T(8,128)(2,1)}), bf16[32,32,128]{2,1,0:T(8,128)(2,1)}, u32[]{:S(2)}, u32[]{:S(2)}) async-start(bf16[32,32,128]{2,1,0:T(8,128)(2,1)} %get-tuple-element.2246), calls=%async_computation.1 | async-start | bytes 524288 | tf_op jit(solution)/shard_map/all_to_all | solution.py:40
  57.5 19.0 %all-to-all-start.3 = ((bf16[32,32,256]{2,1,0:T(8,128)(2,1)}), bf16[32,32,256]{2,1,0:T(8,128)(2,1)S(1)}, u32[]{:S(2)}, u32[]{:S(2)}) async-start(bf16[32,32,256]{2,1,0:T(8,128)(2,1)} %get-tuple-element.2244), calls=%async_computation.3 | async-start | bytes 1048576 | tf_op jit(solution)/shard_map/all_to_all | solution.py:40
  80.0 74.1 %collective-permute-start = (bf16[2048,1,2,128]{3,2,0,1:T(2,128)(2,1)}, bf16[2048,1,2,128]{3,2,0,1:T(2,128)(2,1)}, u32[]{:S(2)}, u32[]{:S(2)}) collective-permute-start(bf16[2048,1,2,128]{3,2,0,1:T(2,128)(2,1)} %reshape_reshape.7), channel_id=1, source_target_pairs={{0,1},{1,2},{2,3},{3,4},{4,5},{5,6},{6,7},{7,0},{8,9},{9,10},{10,1... | collective-permute-start | bytes 3145736 | tf_op jit(solution)/shard_map/ppermute | solution.py:47
  156.5 65.7 %collective-permute-start.1 = (bf16[2048,1,2,128]{3,2,0,1:T(2,128)(2,1)}, bf16[2048,1,2,128]{3,2,0,1:T(2,128)(2,1)}, u32[]{:S(2)}, u32[]{:S(2)}) collective-permute-start(bf16[2048,1,2,128]{3,2,0,1:T(2,128)(2,1)} %collective-permute-done), channel_id=1, source_target_pairs={{0,1},{1,2},{2,3},{3,4},{4,5},{5,6},{6,7},{7,0},{8,9},{9,10},{10,1... | collective-permute-start | bytes 3145736 | tf_op jit(solution)/shard_map/ppermute | solution.py:47
  224.5 67.3 %collective-permute-start.2 = (bf16[2048,1,2,128]{3,2,0,1:T(2,128)(2,1)}, bf16[2048,1,2,128]{3,2,0,1:T(2,128)(2,1)}, u32[]{:S(2)}, u32[]{:S(2)}) collective-permute-start(bf16[2048,1,2,128]{3,2,0,1:T(2,128)(2,1)} %collective-permute-done.1), channel_id=1, source_target_pairs={{0,1},{1,2},{2,3},{3,4},{4,5},{5,6},{6,7},{7,0},{8,9},{9,10},{10,1... | collective-permute-start | bytes 3145736 | tf_op jit(solution)/shard_map/ppermute | solution.py:47
  294.2 65.7 %collective-permute-start.3 = (bf16[2048,1,2,128]{3,2,0,1:T(2,128)(2,1)}, bf16[2048,1,2,128]{3,2,0,1:T(2,128)(2,1)}, u32[]{:S(2)}, u32[]{:S(2)}) collective-permute-start(bf16[2048,1,2,128]{3,2,0,1:T(2,128)(2,1)} %collective-permute-done.2), channel_id=1, source_target_pairs={{0,1},{1,2},{2,3},{3,4},{4,5},{5,6},{6,7},{7,0},{8,9},{9,10},{10,1... | collective-permute-start | bytes 3145736 | tf_op jit(solution)/shard_map/ppermute | solution.py:47
  362.2 67.0 %collective-permute-start.4 = (bf16[2048,1,2,128]{3,2,0,1:T(2,128)(2,1)}, bf16[2048,1,2,128]{3,2,0,1:T(2,128)(2,1)}, u32[]{:S(2)}, u32[]{:S(2)}) collective-permute-start(bf16[2048,1,2,128]{3,2,0,1:T(2,128)(2,1)} %collective-permute-done.3), channel_id=1, source_target_pairs={{0,1},{1,2},{2,3},{3,4},{4,5},{5,6},{6,7},{7,0},{8,9},{9,10},{10,1... | collective-permute-start | bytes 3145736 | tf_op jit(solution)/shard_map/ppermute | solution.py:47
  431.6 65.7 %collective-permute-start.5 = (bf16[2048,1,2,128]{3,2,0,1:T(2,128)(2,1)}, bf16[2048,1,2,128]{3,2,0,1:T(2,128)(2,1)}, u32[]{:S(2)}, u32[]{:S(2)}) collective-permute-start(bf16[2048,1,2,128]{3,2,0,1:T(2,128)(2,1)} %collective-permute-done.4), channel_id=1, source_target_pairs={{0,1},{1,2},{2,3},{3,4},{4,5},{5,6},{6,7},{7,0},{8,9},{9,10},{10,1... | collective-permute-start | bytes 3145736 | tf_op jit(solution)/shard_map/ppermute | solution.py:47
  499.7 66.0 %collective-permute-start.6 = (bf16[2048,1,2,128]{3,2,0,1:T(2,128)(2,1)}, bf16[2048,1,2,128]{3,2,0,1:T(2,128)(2,1)}, u32[]{:S(2)}, u32[]{:S(2)}) collective-permute-start(bf16[2048,1,2,128]{3,2,0,1:T(2,128)(2,1)} %collective-permute-done.5), channel_id=1, source_target_pairs={{0,1},{1,2},{2,3},{3,4},{4,5},{5,6},{6,7},{7,0},{8,9},{9,10},{10,1... | collective-permute-start | bytes 3145736 | tf_op jit(solution)/shard_map/ppermute | solution.py:47
where the time goes:
time: 666 us; the launch traced here: 656 us
  matrix products  215 us (32%)
  local copies, waits for them, and re-layouts  194 us (29%)
  other arithmetic  142 us (21%)
  blocking collectives  60.8 us (9%)
  starting transfers between devices  21.5 us (3%)
  waiting for transfers between devices  18.6 us (3%)
    dot_general x80, matrix products, per_key(): jnp.einsum('cgts,scd->cgtd', weights.astype(jnp.bfloat16), kv_part[:, :,...  117 us
    dot_general x80, matrix products, per_key(): jnp.einsum('cgtd,scd->cgts', q_part, kv_part[:, :, 0, :], preferred_eleme...  97.9 us
    reduce_sum x80, other arithmetic, per_key(): total = total * factor + jnp.sum(weights, axis=-1)  72.1 us
    dynamic_slice x80, local copies, waits for them, and re-layouts, per_key(): k_where = lax.dynamic_slice_in_dim(key_where, start, tile_rows, 0)  60.4 us
    add x80, other arithmetic, per_key(): total = total * factor + jnp.sum(weights, axis=-1)  46.8 us
    dynamic_slice x32, local copies, waits for them, and re-layouts, per_query(): q_where = lax.dynamic_slice_in_dim(query_where, first, tile_rows, 0)  42 us
    all_to_all x2, blocking collectives, several_exchanges(): lax.all_to_all(share, axis, split_axis=0, concat_axis=0, tiled=True)  40.3 us
    dynamic_slice x32, local copies, waits for them, and re-layouts, per_query(): lax.dynamic_slice_in_dim(maxima, first, tile_rows, 2)  22 us
  transfers between devices with their start and end apart: 9, of which 2 were waited for; matrix products, arithmetic and copies ran while one was open for 70% of the time, Pallas kernels for 0%

commit v1 on v0

v1 whole, which is shorter than its diff:
```python
import functools
import math

import jax
import jax.numpy as jnp
import numpy as np
from jax import lax
from jax.experimental import pallas as pl
from jax.experimental.pallas import tpu as pltpu
from jax.sharding import Mesh, PartitionSpec as P


KV_HEADS = 8
GROUP = 4
HEAD_DIM = 128
SPANS = 8
SIDE = 4
MASKED = -1e30
PLANE = ("x", "y", "c")
HOPS = (1, 3, 2)

UNITS = [[(s, s) for s in range(4)], [(s, s) for s in range(4, 8)]]
_used = [0] * SPANS
for _spans in ((7, 6, 5, 4), (7, 6, 5, 4), (7, 6, 5, 4), (7, 6, 5, 4), (7, 6, 5, 3), (7, 6, 3, 2), (7, 3, 2, 1)):
    UNITS.append([(s, _used[s]) for s in _spans])
    for s in _spans:
        _used[s] += 1
assert _used == list(range(SPANS))
WIDE = 4
EXTRA = 16


def turn_kernel(table_ref, place_ref, q_ref, own_ref, partner_ref, *rest, kinds, first, last):
    if first:
        acc_ref, top_ref = rest[:2]
        rest = rest[2:]
    elif last:
        acc_ref, top_ref, out_ref = rest[:3]
        rest = rest[3:]
    else:
        _, _, acc_ref, top_ref = rest[:4]
        rest = rest[4:]
    turned_ref = rest[0]
    slots = (rest[1:4], rest[4:7])
    toks = q_ref.shape[1]
    rows = GROUP * toks
    part = own_ref.shape[0] * toks
    keys = 2 * part
    to_log2 = math.log2(math.e) / math.sqrt(HEAD_DIM)
    x, y, c = (place_ref[n] for n in range(3))

    def columns(span, lo):
        return jnp.concatenate(
            [k[:, span, :, pl.ds(lo, HEAD_DIM)].reshape(part, HEAD_DIM) for k in (own_ref, partner_ref)], axis=0
        )

    if first:
        acc_ref[...] = jnp.zeros_like(acc_ref)
        top_ref[...] = jnp.full_like(top_ref, MASKED)
    for span in range(SPANS):
        turned_ref[span, pl.ds(0, HEAD_DIM)] = columns(span, HEAD_DIM).T
        turned_ref[span, pl.ds(HEAD_DIM, EXTRA)] = jnp.ones((EXTRA, keys), jnp.bfloat16)

    place = (x * SIDE + y) * 2 + c
    ahead = lax.broadcasted_iota(jnp.int32, (toks, rows), 0) - lax.broadcasted_iota(jnp.int32, (toks, rows), 1) % toks

    def hide(s):
        pieces = []
        for n in range(keys // toks):
            mine, stage = kinds[n // SIDE]
            core = c if mine else 1 - c
            step = ((0,) + HOPS)[n % SIDE]
            near = (jnp.where(core == 0, x, y) + (SIDE - step)) % SIDE
            far = (jnp.where(core == 0, y, x) + (SIDE - stage)) % SIDE
            chip = jnp.where(core == 0, near * SIDE + far, far * SIDE + near)
            start = (chip * 2 + core - place) * toks
            pieces.append(jnp.where(ahead <= -start, s[n * toks : (n + 1) * toks], MASKED))
        return jnp.concatenate(pieces, axis=0)

    def scores(unit, t, slot, diagonal):
        score, shift, gain = slot
        tile = table_ref[0, unit * WIDE + t]
        span = table_ref[1, unit * WIDE + t]
        q = jnp.concatenate([q_ref[tile, :, pl.ds(h * HEAD_DIM, HEAD_DIM)] for h in range(GROUP)], axis=0)
        s = lax.dot_general(columns(span, 0), q, (((1,), (1,)), ((), ())), preferred_element_type=jnp.float32)
        if diagonal:
            s = hide(s)
        score[t] = s
        old = top_ref[tile]
        high = jnp.max(s.reshape(keys // 8, 8, rows), axis=0)
        new = jnp.maximum(old, jnp.broadcast_to(jnp.max(high, axis=0, keepdims=True), old.shape))
        top_ref[tile] = new
        shift[t] = new * to_log2
        gain[t] = jnp.exp2((old - new) * to_log2)

    def gather(unit, t, slot):
        score, shift, gain = slot
        tile = table_ref[0, unit * WIDE + t]
        span = table_ref[1, unit * WIDE + t]
        less = shift[t, 0:1]
        w = jnp.exp2(score[t] * to_log2 - less).astype(jnp.bfloat16)
        more = jnp.dot(turned_ref[span], w, preferred_element_type=jnp.float32)
        acc_ref[tile] = acc_ref[tile] * gain[t, 0:1] + more

    count = len(UNITS)

    def both(up, down):
        for t in range(WIDE):
            if up is not None:
                scores(up[0], t, slots[up[1]], up[2])
            if down is not None:
                gather(down[0], t, slots[down[1]])

    both((0, 0, True), None)
    both((1, 1, True), (0, 0))

    def two(i, carry):
        both((2 * i + 2, 0, False), (2 * i + 1, 1))
        both((2 * i + 3, 1, False), (2 * i + 2, 0))
        return carry

    lax.fori_loop(0, (count - 3) // 2, two, 0)
    both((count - 1, 0, False), (count - 2, 1))
    both(None, (count - 1, 0))
    if last:
        for tile in range(SPANS):
            mixed = (acc_ref[tile, pl.ds(0, HEAD_DIM)] / acc_ref[tile, pl.ds(HEAD_DIM, 1)]).T.astype(jnp.bfloat16)
            for h in range(GROUP):
                out_ref[tile, :, pl.ds(h * HEAD_DIM, HEAD_DIM)] = mixed[h * toks : (h + 1) * toks]


def turn(kinds, place, q, own, partner, state, last):
    tiles, toks, _ = q.shape
    rows = GROUP * toks
    first = state is None
    vmem = pl.BlockSpec(memory_space=pltpu.VMEM)
    smem = pl.BlockSpec(memory_space=pltpu.SMEM)
    keys = SIDE * 2 * toks
    state_shape = [
        jax.ShapeDtypeStruct((tiles, HEAD_DIM + EXTRA, rows), jnp.float32),
        jax.ShapeDtypeStruct((tiles, 8, rows), jnp.float32),
    ]
    out_shape = jax.ShapeDtypeStruct(q.shape, jnp.bfloat16) if last else state_shape
    slot = [
        pltpu.VMEM((WIDE, keys, rows), jnp.float32),
        pltpu.VMEM((WIDE, 8, rows), jnp.float32),
        pltpu.VMEM((WIDE, 8, rows), jnp.float32),
    ]
    table = jnp.asarray(np.array(UNITS, np.int32).reshape(-1, 2).T)
    scores = len(UNITS) * WIDE * rows * keys
    return pl.pallas_call(
        functools.partial(turn_kernel, kinds=kinds, first=first, last=last),
        in_specs=[smem, smem] + [vmem] * (3 if first else 5),
        out_specs=vmem if last else [vmem, vmem],
        out_shape=out_shape,
        scratch_shapes=[pltpu.VMEM((SPANS, HEAD_DIM + EXTRA, keys), jnp.bfloat16)] + slot + slot,
        input_output_aliases={} if first or last else {5: 0, 6: 1},
        compiler_params=pltpu.CompilerParams(vmem_limit_bytes=40 * 2**20),
        cost_estimate=pl.CostEstimate(flops=4 * scores * HEAD_DIM, bytes_accessed=8 * 2**20, transcendentals=scores),
    )(table, place, q, own, partner, *(() if first else state))


def hop(value, steps, phase):
    pairs = []
    for x in range(SIDE):
        for y in range(SIDE):
            for c in range(2):
                to = ((x + steps) % SIDE, y) if c == phase else (x, (y + steps) % SIDE)
                pairs.append(((x * SIDE + y) * 2 + c, (to[0] * SIDE + to[1]) * 2 + c))
    return lax.ppermute(value, PLANE, pairs)


def swap(value):
    return lax.ppermute(value, "c", [(0, 1), (1, 0)])


def after(value, *others):
    return lax.optimization_barrier((value, *others))[0]


def per_device(queries, key_rows, value_rows):
    toks = queries.shape[0]
    cols = GROUP * HEAD_DIM
    kv = jnp.concatenate(
        (key_rows.reshape(toks, KV_HEADS, HEAD_DIM), value_rows.reshape(toks, KV_HEADS, HEAD_DIM)), axis=2
    ).transpose(1, 0, 2)
    kv = lax.all_to_all(kv, "z", 0, 0, tiled=True)[None]
    q = queries.reshape(toks, KV_HEADS, cols).transpose(1, 0, 2)
    q = lax.all_to_all(q, "z", 0, 0, tiled=True)
    near = []
    for k in HOPS:
        near.append(hop(kv, k, 0))
    own = [jnp.concatenate([kv] + near, axis=0)]

    def far(k, *before):
        return hop(after(own[0], *before) if before else own[0], k, 1)

    own += [far(k) for k in HOPS[:2]]
    place = jnp.stack([lax.axis_index(a) for a in PLANE]).astype(jnp.int32)

    def swapped(n, *before):
        return swap(after(own[n], *before) if before else own[n])

    def turned(n, first, second, a, b, state):
        return turn((first, second), place, q, a, b, state, n == 3)

    partner = [swapped(0)]
    state = turned(0, (True, 0), (False, 0), own[0], partner[0], None)
    own.append(far(HOPS[2], *state))
    partner += [swapped(1, *state), swapped(2, *state)]
    state = turned(1, (True, HOPS[0]), (True, HOPS[1]), own[1], own[2], state)
    state = turned(2, (False, HOPS[0]), (False, HOPS[1]), partner[1], partner[2], state)
    partner.append(swapped(3, *state))
    out = turned(3, (True, HOPS[2]), (False, HOPS[2]), own[3], partner[3], state)
    out = lax.all_to_all(out, "z", 0, 0, tiled=True)
    return out.transpose(1, 0, 2).reshape(toks, KV_HEADS * cols)


def solution(mesh):
    grid = Mesh(mesh.devices.reshape(8, 4, 4, 2), ("z", "x", "y", "c"))
    spec = P(("z", "x", "y", "c"), None)
    return jax.shard_map(per_device, mesh=grid, in_specs=(spec,) * 3, out_specs=spec, check_vma=False)
```

time: 666 us -> 112 us (0.17); the launches traced: 656 us -> 111 us
  matrix products: 215 us -> 0 us
  local copies, waits for them, and re-layouts: 194 us -> 3.56 us
  other arithmetic: 142 us -> 0.24 us
  Pallas kernels: 0 us -> 25.7 us
  blocking collectives: 60.8 us -> 39.6 us
  waiting for transfers between devices: 18.6 us -> 25.9 us
    dot_general x160 -> x0, matrix products: 215 us -> none  [the longest x80 117 us: per_key(): jnp.einsum('cgts,scd->cgtd', weights.astype(jnp.bfloat16), kv_part[:, :,...]
    dynamic_slice x240 -> x0, local copies, waits for them, and re-layouts: 147 us -> none  [the longest x80 60.4 us: per_key(): k_where = lax.dynamic_slice_in_dim(key_where, start, tile_rows, 0)]
    reduce_sum x80 -> x0, other arithmetic: 72.1 us -> none  [per_key(): total = total * factor + jnp.sum(weights, axis=-1)]
    add x113 -> x0, other arithmetic: 66.8 us -> none  [the longest x80 46.8 us: per_key(): total = total * factor + jnp.sum(weights, axis=-1)]
    pallas_call x0 -> x4, Pallas kernels: none -> 25.7 us  [turn(): pl.pallas_call(functools.partial(turn_kernel, kinds=kinds, first=first, l...]
    all_to_all x3 -> x2, blocking collectives: 60.8 us -> 39.6 us  [the longest x1 20.3 us: per_device(): out = lax.all_to_all(out, 'z', 0, 0, tiled=True)]
    dynamic_update_slice x64 -> x0, local copies, waits for them, and re-layouts: 19.8 us -> none  [the longest x32 19 us: per_query(): totals = lax.dynamic_update_slice_in_dim(totals, total, first, 2)]
    unnamed x16 -> x6, local copies, waits for them, and re-layouts: 19.9 us -> 0.91 us
  transfers between devices with their start and end apart: 9 -> 11, of which waited for: 2 -> 5; matrix products, arithmetic and copies ran while one was open for 70% -> 1% of each run, Pallas kernels for 0% -> 17%
where the time goes in v1:
time: 112 us; the launch traced here: 111 us
  blocking collectives  39.6 us (35%)
  waiting for transfers between devices  25.9 us (23%)
  Pallas kernels  25.7 us (23%)
  starting transfers between devices  16.1 us (14%)
  local copies, waits for them, and re-layouts  3.56 us (3%)
    pallas_call x4, Pallas kernels, turn(): pl.pallas_call(functools.partial(turn_kernel, kinds=kinds, first=first, l...  25.7 us
    all_to_all x1, blocking collectives, per_device(): out = lax.all_to_all(out, 'z', 0, 0, tiled=True)  20.3 us
    all_to_all x1, blocking collectives, per_device(): kv = lax.all_to_all(kv, 'z', 0, 0, tiled=True)[None]  19.3 us
    all_to_all x1, waiting for transfers between devices, per_device(): q = lax.all_to_all(q, 'z', 0, 0, tiled=True)  15.8 us
    ppermute x6, waiting for transfers between devices, hop(): return lax.ppermute(value, PLANE, pairs)  7.81 us
    ppermute x6, starting transfers between devices, hop(): return lax.ppermute(value, PLANE, pairs)  7.71 us
    ppermute x4, starting transfers between devices, swap(): return lax.ppermute(value, 'c', [(0, 1), (1, 0)])  4.91 us
    all_to_all x1, starting transfers between devices, per_device(): q = lax.all_to_all(q, 'z', 0, 0, tiled=True)  3.49 us
  transfers between devices with their start and end apart: 11, of which 5 were waited for; matrix products, arithmetic and copies ran while one was open for 1% of the time, Pallas kernels for 17%

profile of v1, /device:TPU:1, one launch (start us, length us, event | category | flops | bytes accessed | tf_op | source)
XLA Modules:
  0.0 111.3 jit_solution(18001297722326179061)
XLA Ops:
  0.0 0.0 copy-start
  0.0 0.9 copy-done
  0.9 1.0 copy_bitcast_fusion
  1.9 19.3 %all_to_all.15 = bf16[8,64,256]{2,1,0:T(8,128)(2,1)S(1)} all-to-all(bf16[8,64,256]{2,1,0:T(8,128)(2,1)S(1)} %maximum_bitcast_fusion), channel_id=1, replica_groups=mesh['z'=8,'x'=4,'y'=4,'c'=2] {'z'}, dimensions={0} | all-to-all | bytes 524288 | tf_op jit(solution)/shard_map/all_to_all | solution.py:187
  21.2 0.0 copy-start.2
  21.2 1.3 %collective-permute-start = (bf16[1,8,64,256]{3,2,1,0:T(8,128)(2,1)S(1)}, bf16[1,8,64,256]{3,2,1,0:T(8,128)(2,1)S(1)}, u32[]{:S(2)}, u32[]{:S(2)}) collective-permute-start(bf16[1,8,64,256]{3,2,1,0:T(8,128)(2,1)S(1)} %bitcast.27), channel_id=1, source_target_pairs={{0,8},{1,3},{2,10},{3,5},{4,12},{5,7},{6,14},{7,1},{8,16},{9,11},{... | collective-permute-start | bytes 786440 | tf_op jit(solution)/shard_map/ppermute | solution.py:170
  22.5 1.4 %collective-permute-start.1 = (bf16[1,8,64,256]{3,2,1,0:T(8,128)(2,1)S(1)}, bf16[1,8,64,256]{3,2,1,0:T(8,128)(2,1)S(1)}, u32[]{:S(2)}, u32[]{:S(2)}) collective-permute-start(bf16[1,8,64,256]{3,2,1,0:T(8,128)(2,1)S(1)} %bitcast.28), channel_id=1, source_target_pairs={{0,24},{1,7},{2,26},{3,1},{4,28},{5,3},{6,30},{7,5},{8,0},{9,15},{... | collective-permute-start | bytes 786440 | tf_op jit(solution)/shard_map/ppermute | solution.py:170
  24.0 1.6 %collective-permute-start.2 = (bf16[1,8,64,256]{3,2,1,0:T(8,128)(2,1)S(1)}, bf16[1,8,64,256]{3,2,1,0:T(8,128)(2,1)S(1)}, u32[]{:S(2)}, u32[]{:S(2)}) collective-permute-start(bf16[1,8,64,256]{3,2,1,0:T(8,128)(2,1)S(1)} %bitcast.29), channel_id=1, source_target_pairs={{0,16},{1,5},{2,18},{3,7},{4,20},{5,1},{6,22},{7,3},{8,24},{9,13},... | collective-permute-start | bytes 786440 | tf_op jit(solution)/shard_map/ppermute | solution.py:170
  25.6 2.4 %collective-permute-done = bf16[1,8,64,256]{3,2,1,0:T(8,128)(2,1)S(1)} collective-permute-done((bf16[1,8,64,256]{3,2,1,0:T(8,128)(2,1)S(1)}, bf16[1,8,64,256]{3,2,1,0:T(8,128)(2,1)S(1)}, u32[]{:S(2)}, u32[]{:S(2)}) %collective-permute-start) | collective-permute-done | bytes 262176 | tf_op jit(solution)/shard_map/ppermute | solution.py:170
  28.0 0.0 collective-permute-done.1
  28.0 4.0 %collective-permute-done.2 = bf16[1,8,64,256]{3,2,1,0:T(8,128)(2,1)S(1)} collective-permute-done((bf16[1,8,64,256]{3,2,1,0:T(8,128)(2,1)S(1)}, bf16[1,8,64,256]{3,2,1,0:T(8,128)(2,1)S(1)}, u32[]{:S(2)}, u32[]{:S(2)}) %collective-permute-start.2) | collective-permute-done | bytes 262176 | tf_op jit(solution)/shard_map/ppermute | solution.py:170
  32.0 0.1 pad_maximum_fusion.own_ref
  32.1 0.0 copy-start.1
  32.1 3.0 %collective-permute-start.3 = (bf16[4,8,64,256]{3,2,1,0:T(8,128)(2,1)S(1)}, bf16[4,8,64,256]{3,2,1,0:T(8,128)(2,1)}, u32[]{:S(2)}, u32[]{:S(2)}) collective-permute-start(bf16[4,8,64,256]{3,2,1,0:T(8,128)(2,1)S(1)} %pad_maximum_fusion.own_ref), channel_id=1, source_target_pairs={{0,1},{1,0},{2,3},{3,2},{4,5},{5,4},{6,7},{7,6},{8,9},{9,8},{10,11... | collective-permute-start | bytes 3145736 | tf_op jit(solution)/shard_map/ppermute | solution.py:174
  35.2 0.0 copy-done.2
  35.2 0.8 copy.23
  36.0 3.5 %all-to-all-start = ((bf16[8,64,512]{2,1,0:T(8,128)(2,1)}), bf16[8,64,512]{2,1,0:T(8,128)(2,1)S(1)}, u32[]{:S(2)}, u32[]{:S(2)}) async-start(bf16[8,64,512]{2,1,0:T(8,128)(2,1)} %bitcast.25), calls=%async_computation | async-start | bytes 1048576 | tf_op jit(solution)/shard_map/all_to_all | solution.py:189
  39.5 2.1 %collective-permute-start.7 = (bf16[4,8,64,256]{3,2,1,0:T(8,128)(2,1)S(1)}, bf16[4,8,64,256]{3,2,1,0:T(8,128)(2,1)S(1)}, u32[]{:S(2)}, u32[]{:S(2)}) collective-permute-start(bf16[4,8,64,256]{3,2,1,0:T(8,128)(2,1)S(1)} %pad_maximum_fusion.own_ref), channel_id=1, source_target_pairs={{0,6},{1,25},{2,0},{3,27},{4,2},{5,29},{6,4},{7,31},{8,14},{9,1},{... | collective-permute-start | bytes 3145736 | tf_op jit(solution)/shard_map/ppermute | solution.py:170
  41.6 0.0 collective-permute-start.5
  41.6 0.1 pad_add_fusion.place_ref
  41.6 15.8 %all-to-all-done.q_ref = bf16[8,64,512]{2,1,0:T(8,128)(2,1)S(1)} async-done(((bf16[8,64,512]{2,1,0:T(8,128)(2,1)}), bf16[8,64,512]{2,1,0:T(8,128)(2,1)S(1)}, u32[]{:S(2)}, u32[]{:S(2)}) %all-to-all-start) | async-done | bytes 524320 | tf_op jit(solution)/shard_map/all_to_all | solution.py:189
  57.5 0.0 collective-permute-done.3.partner_ref
  57.5 0.0 copy-done.1
  57.5 6.7 %shard_map.73 = (f32[8,144,256]{2,1,0:T(8,128)S(1)}, f32[8,8,256]{2,1,0:T(8,128)S(1)}) custom-call(s32[2,36]{1,0:T(2,128)S(1)} %copy-done.1, s32[3]{0:T(128)S(1)} %pad_add_fusion.place_ref, bf16[8,64,512]{2,1,0:T(8,128)(2,1)S(1)} %all-to-all-done.q_ref, bf16[4,8,64,256]{3,2,1,0:T(8,128)(2,1)S(1)} %pad_maximum_fusion.own_ref, ...), custom_call_target="tpu_custom_call" | custom-call | flops 2415919104 | bytes 8388608 | tf_op jit(solution)/shard_map/pallas_call | solution.py:151
  64.2 0.0 collective-permute-done.7.partner_ref
  64.2 0.0 collective-permute-done.5.own_ref
  64.2 0.5 collective-permute-start.8
  64.7 0.1 collective-permute-start.6
  64.8 1.3 %collective-permute-start.4 = (bf16[4,8,64,256]{3,2,1,0:T(8,128)(2,1)S(1)}, bf16[4,8,64,256]{3,2,1,0:T(8,128)(2,1)S(1)}, u32[]{:S(2)}, u32[]{:S(2)}) collective-permute-start(bf16[4,8,64,256]{3,2,1,0:T(8,128)(2,1)S(1)} %pad_maximum_fusion.own_ref), channel_id=1, source_target_pairs={{0,4},{1,17},{2,6},{3,19},{4,0},{5,21},{6,2},{7,23},{8,12},{9,25},... | collective-permute-start | bytes 3145736 | tf_op jit(solution)/shard_map/ppermute | solution.py:170
  66.1 6.7 %shard_map.74 = (f32[8,144,256]{2,1,0:T(8,128)S(1)}, f32[8,8,256]{2,1,0:T(8,128)S(1)}) custom-call(s32[2,36]{1,0:T(2,128)S(1)} %copy-done.1, s32[3]{0:T(128)S(1)} %pad_add_fusion.place_ref, bf16[8,64,512]{2,1,0:T(8,128)(2,1)S(1)} %all-to-all-done.q_ref, ...), custom_call_target="tpu_custom_call", output_to_operand_aliasing={{0}: (5, {}), {1}: (6, {})} | custom-call | flops 2415919104 | bytes 8388608 | tf_op jit(solution)/shard_map/pallas_call | solution.py:151
  72.8 0.0 collective-permute-done.8.partner_ref
  72.8 0.0 collective-permute-done.6.own_ref
  72.8 6.1 %shard_map.75 = (f32[8,144,256]{2,1,0:T(8,128)S(1)}, f32[8,8,256]{2,1,0:T(8,128)S(1)}) custom-call(s32[2,36]{1,0:T(2,128)S(1)} %copy-done.1, s32[3]{0:T(128)S(1)} %pad_add_fusion.place_ref, bf16[8,64,512]{2,1,0:T(8,128)(2,1)S(1)} %all-to-all-done.q_ref, ...), custom_call_target="tpu_custom_call", output_to_operand_aliasing={{0}: (5, {}), {1}: (6, {})} | custom-call | flops 2415919104 | bytes 8388608 | tf_op jit(solution)/shard_map/pallas_call | solution.py:151
  78.9 1.4 %collective-permute-done.4.own_ref = bf16[4,8,64,256]{3,2,1,0:T(8,128)(2,1)S(1)} collective-permute-done((bf16[4,8,64,256]{3,2,1,0:T(8,128)(2,1)S(1)}, bf16[4,8,64,256]{3,2,1,0:T(8,128)(2,1)S(1)}, u32[]{:S(2)}, u32[]{:S(2)}) %collective-permute-start.4) | collective-permute-done | bytes 1048608 | tf_op jit(solution)/shard_map/ppermute | solution.py:170
  80.3 1.3 %collective-permute-start.9 = (bf16[4,8,64,256]{3,2,1,0:T(8,128)(2,1)S(1)}, bf16[4,8,64,256]{3,2,1,0:T(8,128)(2,1)S(1)}, u32[]{:S(2)}, u32[]{:S(2)}) collective-permute-start(bf16[4,8,64,256]{3,2,1,0:T(8,128)(2,1)S(1)} %collective-permute-done.4.own_ref), channel_id=1, source_target_pairs={{0,1},{1,0},{2,3},{3,2},{4,5},{5,4},{6,7},{7,6},{8,9},{9,8},{10,11... | collective-permute-start | bytes 3145736 | tf_op jit(solution)/shard_map/ppermute | solution.py:174
  81.6 2.3 %collective-permute-done.9.partner_ref = bf16[4,8,64,256]{3,2,1,0:T(8,128)(2,1)S(1)} collective-permute-done((bf16[4,8,64,256]{3,2,1,0:T(8,128)(2,1)S(1)}, bf16[4,8,64,256]{3,2,1,0:T(8,128)(2,1)S(1)}, u32[]{:S(2)}, u32[]{:S(2)}) %collective-permute-start.9) | collective-permute-done | bytes 1048608 | tf_op jit(solution)/shard_map/ppermute | solution.py:174
  83.8 6.3 %shard_map.76 = bf16[8,64,512]{2,1,0:T(8,128)(2,1)S(1)} custom-call(s32[2,36]{1,0:T(2,128)S(1)} %copy-done.1, s32[3]{0:T(128)S(1)} %pad_add_fusion.place_ref, bf16[8,64,512]{2,1,0:T(8,128)(2,1)S(1)} %all-to-all-done.q_ref, bf16[4,8,64,256]{3,2,1,0:T(8,128)(2,1)S(1)} %collective-permute-done.4.own_ref, ...), custom_call_target="tpu_custom_call" | custom-call | flops 2415919104 | bytes 8388608 | tf_op jit(solution)/shard_map/pallas_call | solution.py:151
  90.1 20.3 %all_to_all.16 = bf16[8,64,512]{2,1,0:T(8,128)(2,1)S(1)} all-to-all(bf16[8,64,512]{2,1,0:T(8,128)(2,1)S(1)} %shard_map.76), channel_id=1, replica_groups=mesh['z'=8,'x'=4,'y'=4,'c'=2] {'z'}, dimensions={0} | all-to-all | bytes 1048576 | tf_op jit(solution)/shard_map/all_to_all | solution.py:215
  110.4 0.8 copy.19
  (1 shorter events, 0.0 us)
Async XLA Ops:
  0.0 0.9 copy-start
  21.2 14.0 %copy-start.2 = (bf16[64,4096]{1,0:T(8,128)(2,1)S(1)}, bf16[64,4096]{1,0:T(8,128)(2,1)}, u32[]{:S(2)}) copy-start(bf16[64,4096]{1,0:T(8,128)(2,1)} %param.7) | copy-start | bytes 1572868
  21.2 6.8 %collective-permute-start = (bf16[1,8,64,256]{3,2,1,0:T(8,128)(2,1)S(1)}, bf16[1,8,64,256]{3,2,1,0:T(8,128)(2,1)S(1)}, u32[]{:S(2)}, u32[]{:S(2)}) collective-permute-start(bf16[1,8,64,256]{3,2,1,0:T(8,128)(2,1)S(1)} %bitcast.27), channel_id=1, source_target_pairs={{0,8},{1,3},{2,10},{3,5},{4,12},{5,7},{6,14},{7,1},{8,16},{9,11},{... | collective-permute-start | bytes 786440 | tf_op jit(solution)/shard_map/ppermute | solution.py:170
  22.5 5.5 %collective-permute-start.1 = (bf16[1,8,64,256]{3,2,1,0:T(8,128)(2,1)S(1)}, bf16[1,8,64,256]{3,2,1,0:T(8,128)(2,1)S(1)}, u32[]{:S(2)}, u32[]{:S(2)}) collective-permute-start(bf16[1,8,64,256]{3,2,1,0:T(8,128)(2,1)S(1)} %bitcast.28), channel_id=1, source_target_pairs={{0,24},{1,7},{2,26},{3,1},{4,28},{5,3},{6,30},{7,5},{8,0},{9,15},{... | collective-permute-start | bytes 786440 | tf_op jit(solution)/shard_map/ppermute | solution.py:170
  24.0 8.0 %collective-permute-start.2 = (bf16[1,8,64,256]{3,2,1,0:T(8,128)(2,1)S(1)}, bf16[1,8,64,256]{3,2,1,0:T(8,128)(2,1)S(1)}, u32[]{:S(2)}, u32[]{:S(2)}) collective-permute-start(bf16[1,8,64,256]{3,2,1,0:T(8,128)(2,1)S(1)} %bitcast.29), channel_id=1, source_target_pairs={{0,16},{1,5},{2,18},{3,7},{4,20},{5,1},{6,22},{7,3},{8,24},{9,13},... | collective-permute-start | bytes 786440 | tf_op jit(solution)/shard_map/ppermute | solution.py:170
  32.1 25.4 %copy-start.1 = (s32[2,36]{1,0:T(2,128)S(1)}, s32[2,36]{1,0:T(2,128)}, u32[]{:S(2)}) copy-start(s32[2,36]{1,0:T(2,128)} %constant.13.clone.table_ref) | copy-start | bytes 868
  32.1 25.3 %collective-permute-start.3 = (bf16[4,8,64,256]{3,2,1,0:T(8,128)(2,1)S(1)}, bf16[4,8,64,256]{3,2,1,0:T(8,128)(2,1)}, u32[]{:S(2)}, u32[]{:S(2)}) collective-permute-start(bf16[4,8,64,256]{3,2,1,0:T(8,128)(2,1)S(1)} %pad_maximum_fusion.own_ref), channel_id=1, source_target_pairs={{0,1},{1,0},{2,3},{3,2},{4,5},{5,4},{6,7},{7,6},{8,9},{9,8},{10,11... | collective-permute-start | bytes 3145736 | tf_op jit(solution)/shard_map/ppermute | solution.py:174
  36.0 21.5 %all-to-all-start = ((bf16[8,64,512]{2,1,0:T(8,128)(2,1)}), bf16[8,64,512]{2,1,0:T(8,128)(2,1)S(1)}, u32[]{:S(2)}, u32[]{:S(2)}) async-start(bf16[8,64,512]{2,1,0:T(8,128)(2,1)} %bitcast.25), calls=%async_computation | async-start | bytes 1048576 | tf_op jit(solution)/shard_map/all_to_all | solution.py:189
  39.5 24.7 %collective-permute-start.7 = (bf16[4,8,64,256]{3,2,1,0:T(8,128)(2,1)S(1)}, bf16[4,8,64,256]{3,2,1,0:T(8,128)(2,1)S(1)}, u32[]{:S(2)}, u32[]{:S(2)}) collective-permute-start(bf16[4,8,64,256]{3,2,1,0:T(8,128)(2,1)S(1)} %pad_maximum_fusion.own_ref), channel_id=1, source_target_pairs={{0,6},{1,25},{2,0},{3,27},{4,2},{5,29},{6,4},{7,31},{8,14},{9,1},{... | collective-permute-start | bytes 3145736 | tf_op jit(solution)/shard_map/ppermute | solution.py:170
  41.6 22.6 %collective-permute-start.5 = (bf16[4,8,64,256]{3,2,1,0:T(8,128)(2,1)S(1)}, bf16[4,8,64,256]{3,2,1,0:T(8,128)(2,1)}, u32[]{:S(2)}, u32[]{:S(2)}) collective-permute-start(bf16[4,8,64,256]{3,2,1,0:T(8,128)(2,1)S(1)} %pad_maximum_fusion.own_ref), channel_id=1, source_target_pairs={{0,2},{1,9},{2,4},{3,11},{4,6},{5,13},{6,0},{7,15},{8,10},{9,17},{... | collective-permute-start | bytes 3145736 | tf_op jit(solution)/shard_map/ppermute | solution.py:170
  64.2 8.6 %collective-permute-start.8 = (bf16[4,8,64,256]{3,2,1,0:T(8,128)(2,1)S(1)}, bf16[4,8,64,256]{3,2,1,0:T(8,128)(2,1)S(1)}, u32[]{:S(2)}, u32[]{:S(2)}) collective-permute-start(bf16[4,8,64,256]{3,2,1,0:T(8,128)(2,1)S(1)} %collective-permute-done.7.partner_ref), channel_id=1, source_target_pairs={{0,1},{1,0},{2,3},{3,2},{4,5},{5,4},{6,7},{7,6},{8,9},{9,8},{10,11... | collective-permute-start | bytes 3145736 | tf_op jit(solution)/shard_map/ppermute | solution.py:174
  64.7 8.1 %collective-permute-start.6 = (bf16[4,8,64,256]{3,2,1,0:T(8,128)(2,1)}, bf16[4,8,64,256]{3,2,1,0:T(8,128)(2,1)S(1)}, u32[]{:S(2)}, u32[]{:S(2)}) collective-permute-start(bf16[4,8,64,256]{3,2,1,0:T(8,128)(2,1)} %collective-permute-done.5.own_ref), channel_id=1, source_target_pairs={{0,1},{1,0},{2,3},{3,2},{4,5},{5,4},{6,7},{7,6},{8,9},{9,8},{10,11... | collective-permute-start | bytes 3145736 | tf_op jit(solution)/shard_map/ppermute | solution.py:174
  64.8 15.4 %collective-permute-start.4 = (bf16[4,8,64,256]{3,2,1,0:T(8,128)(2,1)S(1)}, bf16[4,8,64,256]{3,2,1,0:T(8,128)(2,1)S(1)}, u32[]{:S(2)}, u32[]{:S(2)}) collective-permute-start(bf16[4,8,64,256]{3,2,1,0:T(8,128)(2,1)S(1)} %pad_maximum_fusion.own_ref), channel_id=1, source_target_pairs={{0,4},{1,17},{2,6},{3,19},{4,0},{5,21},{6,2},{7,23},{8,12},{9,25},... | collective-permute-start | bytes 3145736 | tf_op jit(solution)/shard_map/ppermute | solution.py:170
  80.3 3.6 %collective-permute-start.9 = (bf16[4,8,64,256]{3,2,1,0:T(8,128)(2,1)S(1)}, bf16[4,8,64,256]{3,2,1,0:T(8,128)(2,1)S(1)}, u32[]{:S(2)}, u32[]{:S(2)}) collective-permute-start(bf16[4,8,64,256]{3,2,1,0:T(8,128)(2,1)S(1)} %collective-permute-done.4.own_ref), channel_id=1, source_target_pairs={{0,1},{1,0},{2,3},{3,2},{4,5},{5,4},{6,7},{7,6},{8,9},{9,8},{10,11... | collective-permute-start | bytes 3145736 | tf_op jit(solution)/shard_map/ppermute | solution.py:174

commit v2 on v1

--- a/solution.py
+++ b/solution.py
@@ -30,7 +30,8 @@
 EXTRA = 16
 
 
-def turn_kernel(table_ref, place_ref, q_ref, own_ref, partner_ref, *rest, kinds, first, last):
+def turn_kernel(table_ref, place_ref, q_ref, *rest, kinds, first, last):
+    parts, rest = rest[: len(kinds)], rest[len(kinds) :]
     if first:
         acc_ref, top_ref = rest[:2]
         rest = rest[2:]
@@ -44,14 +45,14 @@
     slots = (rest[1:4], rest[4:7])
     toks = q_ref.shape[1]
     rows = GROUP * toks
-    part = own_ref.shape[0] * toks
-    keys = 2 * part
+    chips = [(mine, near, far) for mine, steps in kinds for near, far in steps]
+    keys = len(chips) * toks
     to_log2 = math.log2(math.e) / math.sqrt(HEAD_DIM)
     x, y, c = (place_ref[n] for n in range(3))
 
     def columns(span, lo):
         return jnp.concatenate(
-            [k[:, span, :, pl.ds(lo, HEAD_DIM)].reshape(part, HEAD_DIM) for k in (own_ref, partner_ref)], axis=0
+            [k[:, span, :, pl.ds(lo, HEAD_DIM)].reshape(k.shape[0] * toks, HEAD_DIM) for k in parts], axis=0
         )
 
     if first:
@@ -66,12 +67,10 @@
 
     def hide(s):
         pieces = []
-        for n in range(keys // toks):
-            mine, stage = kinds[n // SIDE]
+        for n, (mine, near, far) in enumerate(chips):
             core = c if mine else 1 - c
-            step = ((0,) + HOPS)[n % SIDE]
-            near = (jnp.where(core == 0, x, y) + (SIDE - step)) % SIDE
-            far = (jnp.where(core == 0, y, x) + (SIDE - stage)) % SIDE
+            near = (jnp.where(core == 0, x, y) + (SIDE - near)) % SIDE
+            far = (jnp.where(core == 0, y, x) + (SIDE - far)) % SIDE
             chip = jnp.where(core == 0, near * SIDE + far, far * SIDE + near)
             start = (chip * 2 + core - place) * toks
             pieces.append(jnp.where(ahead <= -start, s[n * toks : (n + 1) * toks], MASKED))
@@ -129,13 +128,13 @@
                 out_ref[tile, :, pl.ds(h * HEAD_DIM, HEAD_DIM)] = mixed[h * toks : (h + 1) * toks]
 
 
-def turn(kinds, place, q, own, partner, state, last):
+def turn(kinds, place, q, parts, state, last):
     tiles, toks, _ = q.shape
     rows = GROUP * toks
     first = state is None
     vmem = pl.BlockSpec(memory_space=pltpu.VMEM)
     smem = pl.BlockSpec(memory_space=pltpu.SMEM)
-    keys = SIDE * 2 * toks
+    keys = sum(p.shape[0] for p in parts) * toks
     state_shape = [
         jax.ShapeDtypeStruct((tiles, HEAD_DIM + EXTRA, rows), jnp.float32),
         jax.ShapeDtypeStruct((tiles, 8, rows), jnp.float32),
@@ -148,16 +147,17 @@
     ]
     table = jnp.asarray(np.array(UNITS, np.int32).reshape(-1, 2).T)
     scores = len(UNITS) * WIDE * rows * keys
+    ahead = 3 + len(parts)
     return pl.pallas_call(
         functools.partial(turn_kernel, kinds=kinds, first=first, last=last),
-        in_specs=[smem, smem] + [vmem] * (3 if first else 5),
+        in_specs=[smem, smem] + [vmem] * (1 + len(parts) + (0 if first else 2)),
         out_specs=vmem if last else [vmem, vmem],
         out_shape=out_shape,
         scratch_shapes=[pltpu.VMEM((SPANS, HEAD_DIM + EXTRA, keys), jnp.bfloat16)] + slot + slot,
-        input_output_aliases={} if first or last else {5: 0, 6: 1},
-        compiler_params=pltpu.CompilerParams(vmem_limit_bytes=40 * 2**20),
+        input_output_aliases={} if first or last else {ahead: 0, ahead + 1: 1},
+        compiler_params=pltpu.CompilerParams(vmem_limit_bytes=12 * 2**20),
         cost_estimate=pl.CostEstimate(flops=4 * scores * HEAD_DIM, bytes_accessed=8 * 2**20, transcendentals=scores),
-    )(table, place, q, own, partner, *(() if first else state))
+    )(table, place, q, *parts, *(() if first else state))
 
 
 def hop(value, steps, phase):
@@ -174,6 +174,31 @@
     return lax.ppermute(value, "c", [(0, 1), (1, 0)])
 
 
+def by_head(key_rows, value_rows):
+    def body(key_ref, value_ref, out_ref, sems):
+        copies = []
+        for g in range(KV_HEADS):
+            lanes = pl.ds(g * HEAD_DIM, HEAD_DIM)
+            for n, ref in enumerate((key_ref, value_ref)):
+                to = out_ref.at[g, :, pl.ds(n * HEAD_DIM, HEAD_DIM)]
+                copies.append(pltpu.make_async_copy(ref.at[:, lanes], to, sems.at[2 * g + n]))
+        for copy in copies:
+            copy.start()
+        for copy in copies:
+            copy.wait()
+
+    hbm = pl.BlockSpec(memory_space=pltpu.HBM)
+    shape = (KV_HEADS, key_rows.shape[0], 2 * HEAD_DIM)
+    return pl.pallas_call(
+        body,
+        in_specs=[hbm, hbm],
+        out_specs=pl.BlockSpec(memory_space=pltpu.VMEM),
+        out_shape=jax.ShapeDtypeStruct(shape, key_rows.dtype),
+        scratch_shapes=[pltpu.SemaphoreType.DMA((2 * KV_HEADS,))],
+        compiler_params=pltpu.CompilerParams(vmem_limit_bytes=60 * 2**20),
+    )(key_rows, value_rows)
+
+
 def after(value, *others):
     return lax.optimization_barrier((value, *others))[0]
 
@@ -181,37 +206,56 @@
 def per_device(queries, key_rows, value_rows):
     toks = queries.shape[0]
     cols = GROUP * HEAD_DIM
-    kv = jnp.concatenate(
-        (key_rows.reshape(toks, KV_HEADS, HEAD_DIM), value_rows.reshape(toks, KV_HEADS, HEAD_DIM)), axis=2
-    ).transpose(1, 0, 2)
+    kv = by_head(key_rows, value_rows)
     kv = lax.all_to_all(kv, "z", 0, 0, tiled=True)[None]
     q = queries.reshape(toks, KV_HEADS, cols).transpose(1, 0, 2)
     q = lax.all_to_all(q, "z", 0, 0, tiled=True)
-    near = []
-    for k in HOPS:
-        near.append(hop(kv, k, 0))
-    own = [jnp.concatenate([kv] + near, axis=0)]
-
-    def far(k, *before):
-        return hop(after(own[0], *before) if before else own[0], k, 1)
-
-    own += [far(k) for k in HOPS[:2]]
+
+    def moved(value, steps, phase, *before):
+        return hop(after(value, *before) if before else value, steps, phase)
+
+    def swapped(value, *before):
+        return swap(after(value, *before) if before else value)
+
+    near = {k: moved(kv, k, 0) for k in HOPS}
+    low = jnp.concatenate([kv, near[1]], axis=0)
+    high = jnp.concatenate([near[3], near[2]], axis=0)
+    low_1 = moved(low, 1, 1)
+    high_3 = moved(high, 3, 1)
+    high_1 = moved(high, 1, 1)
+    low_3 = moved(low, 3, 1)
+    low_p, high_p = swapped(low, q), swapped(high, q)
     place = jnp.stack([lax.axis_index(a) for a in PLANE]).astype(jnp.int32)
 
-    def swapped(n, *before):
-        return swap(after(own[n], *before) if before else own[n])
-
-    def turned(n, first, second, a, b, state):
-        return turn((first, second), place, q, a, b, state, n == 3)
-
-    partner = [swapped(0)]
-    state = turned(0, (True, 0), (False, 0), own[0], partner[0], None)
-    own.append(far(HOPS[2], *state))
-    partner += [swapped(1, *state), swapped(2, *state)]
-    state = turned(1, (True, HOPS[0]), (True, HOPS[1]), own[1], own[2], state)
-    state = turned(2, (False, HOPS[0]), (False, HOPS[1]), partner[1], partner[2], state)
-    partner.append(swapped(3, *state))
-    out = turned(3, (True, HOPS[2]), (False, HOPS[2]), own[3], partner[3], state)
+    low_2, high_2 = moved(low_1, 1, 1), moved(high_3, 3, 1)
+
+    def low_at(far):
+        return ((0, far), (1, far))
+
+    def high_at(far):
+        return ((3, far), (2, far))
+
+    def turned(n, parts, state):
+        kinds = tuple(p[:2] for p in parts)
+        return turn(kinds, place, q, [p[2] for p in parts], state, n == 3)
+
+    state = turned(
+        0, [(True, low_at(0), low), (True, high_at(0), high), (True, low_at(1), low_1), (True, high_at(3), high_3)], None
+    )
+    nearby = [(low_at(1), low_1), (high_at(3), high_3), (high_at(1), high_1), (low_at(3), low_3)]
+    nearby_p = [(False, at, swapped(value, *state)) for at, value in nearby]
+    state = turned(
+        1,
+        [(False, low_at(0), low_p), (False, high_at(0), high_p), (True, high_at(1), high_1), (True, low_at(3), low_3)],
+        state,
+    )
+    low_2p, high_2p = swapped(low_2, *state), swapped(high_2, *state)
+    state = turned(2, nearby_p, state)
+    out = turned(
+        3,
+        [(True, low_at(2), low_2), (True, high_at(2), high_2), (False, low_at(2), low_2p), (False, high_at(2), high_2p)],
+        state,
+    )
     out = lax.all_to_all(out, "z", 0, 0, tiled=True)
     return out.transpose(1, 0, 2).reshape(toks, KV_HEADS * cols)
 

time: 112 us -> 108 us (0.964)
  waiting for transfers between devices: 25.9 us -> 6.98 us
  starting transfers between devices: 16.1 us -> 28.1 us
  blocking collectives: 39.6 us -> 43.3 us
  Pallas kernels: 25.7 us -> 27.6 us
  local copies, waits for them, and re-layouts: 3.56 us -> 1.72 us
    all_to_all x1, waiting for transfers between devices: 15.8 us -> 4.1 us  [per_device(): q = lax.all_to_all(q, 'z', 0, 0, tiled=True)]
    ppermute x4 -> x8, starting transfers between devices: 4.91 us -> 11.3 us  [swap(): return lax.ppermute(value, 'c', [(0, 1), (1, 0)])]
    ppermute x6 -> x9, starting transfers between devices: 7.71 us -> 13.3 us  [hop(): return lax.ppermute(value, PLANE, pairs)]
    ppermute x6 -> x9, waiting for transfers between devices: 7.81 us -> 2.86 us  [hop(): return lax.ppermute(value, PLANE, pairs)]
    all_to_all x1, blocking collectives: 20.3 us -> 23.8 us  [per_device(): out = lax.all_to_all(out, 'z', 0, 0, tiled=True)]
    ppermute x4 -> x8, waiting for transfers between devices: 2.29 us -> 0.02 us  [swap(): return lax.ppermute(value, 'c', [(0, 1), (1, 0)])]
    pallas_call x0 -> x1, Pallas kernels: none -> 1.78 us  [by_head(): pl.pallas_call(body, in_specs=[hbm, hbm], out_specs=pl.BlockSpec(memory_s...]
  transfers between devices with their start and end apart: 11 -> 18, of which waited for: 5 -> 4; matrix products, arithmetic and copies ran while one was open for 1% -> 1% of each run, Pallas kernels for 17% -> 18%
where the time goes in v2:
time: 108 us
  blocking collectives  43.3 us (40%)
  starting transfers between devices  28.1 us (26%)
  Pallas kernels  27.6 us (26%)
  waiting for transfers between devices  6.98 us (6%)
  local copies, waits for them, and re-layouts  1.72 us (2%)
    pallas_call x4, Pallas kernels, turn(): pl.pallas_call(functools.partial(turn_kernel, kinds=kinds, first=first, l...  25.8 us
    all_to_all x1, blocking collectives, per_device(): out = lax.all_to_all(out, 'z', 0, 0, tiled=True)  23.8 us
    all_to_all x1, blocking collectives, per_device(): kv = lax.all_to_all(kv, 'z', 0, 0, tiled=True)[None]  19.5 us
    ppermute x9, starting transfers between devices, hop(): return lax.ppermute(value, PLANE, pairs)  13.3 us
    ppermute x8, starting transfers between devices, swap(): return lax.ppermute(value, 'c', [(0, 1), (1, 0)])  11.3 us
    all_to_all x1, waiting for transfers between devices, per_device(): q = lax.all_to_all(q, 'z', 0, 0, tiled=True)  4.1 us
    all_to_all x1, starting transfers between devices, per_device(): q = lax.all_to_all(q, 'z', 0, 0, tiled=True)  3.49 us
    ppermute x9, waiting for transfers between devices, hop(): return lax.ppermute(value, PLANE, pairs)  2.86 us
  transfers between devices with their start and end apart: 18, of which 4 were waited for; matrix products, arithmetic and copies ran while one was open for 1% of the time, Pallas kernels for 18%

profile of v2, /device:TPU:1, one launch (start us, length us, event | category | flops | bytes accessed | tf_op | source)
XLA Modules:
  0.0 108.0 jit_solution(3283901195555668123)
XLA Ops:
  0.0 0.0 copy-start.1
  0.0 1.8 %shard_map.73 = bf16[8,64,256]{2,1,0:T(8,128)(2,1)} custom-call(bf16[64,1024]{1,0:T(8,128)(2,1)} %key_ref.1, bf16[64,1024]{1,0:T(8,128)(2,1)} %value_ref.1), custom_call_target="tpu_custom_call" | custom-call | tf_op jit(solution)/shard_map/pallas_call | solution.py:192
  1.8 19.5 %all_to_all.15 = bf16[8,64,256]{2,1,0:T(8,128)(2,1)S(1)} all-to-all(bf16[8,64,256]{2,1,0:T(8,128)(2,1)} %shard_map.73), channel_id=1, replica_groups=mesh['z'=8,'x'=4,'y'=4,'c'=2] {'z'}, dimensions={0} | all-to-all | bytes 524288 | tf_op jit(solution)/shard_map/all_to_all | solution.py:210
  21.3 2.7 %collective-permute-start.3 = (bf16[1,8,64,256]{3,2,1,0:T(8,128)(2,1)S(1)}, bf16[1,8,64,256]{3,2,1,0:T(8,128)(2,1)S(1)}, u32[]{:S(2)}, u32[]{:S(2)}) collective-permute-start(bf16[1,8,64,256]{3,2,1,0:T(8,128)(2,1)S(1)} %bitcast.15), channel_id=1, source_target_pairs={{0,24},{1,7},{2,26},{3,1},{4,28},{5,3},{6,30},{7,5},{8,0},{9,15},{... | collective-permute-start | bytes 786440 | tf_op jit(solution)/shard_map/ppermute | solution.py:170
  24.0 0.3 collective-permute-start.4
  24.4 0.0 copy-done.1
  24.4 0.8 copy.17
  25.2 3.5 %all-to-all-start = ((bf16[8,64,512]{2,1,0:T(8,128)(2,1)}), bf16[8,64,512]{2,1,0:T(8,128)(2,1)S(1)}, u32[]{:S(2)}, u32[]{:S(2)}) async-start(bf16[8,64,512]{2,1,0:T(8,128)(2,1)} %bitcast.13), calls=%async_computation | async-start | bytes 1048576 | tf_op jit(solution)/shard_map/all_to_all | solution.py:212
  28.7 0.0 copy-start
  28.7 0.8 collective-permute-start
  29.5 0.6 collective-permute-done.3
  30.2 0.6 collective-permute-done.4
  30.8 2.9 %collective-permute-start.5 = (bf16[2,8,64,256]{3,2,1,0:T(8,128)(2,1)S(1)}, bf16[2,8,64,256]{3,2,1,0:T(8,128)(2,1)S(1)}, u32[]{:S(2)}, u32[]{:S(2)}) collective-permute-start(bf16[2,8,64,256]{3,2,1,0:T(8,128)(2,1)S(1)} %constant_dynamic-update-slice_fusion.rest_1_), channel_id=1, source_target_pairs={{0,6},{1,25},{2,0},{3,27},{4,2},{5,29},{6,4},{7,31},{8,14},{9,1},{... | collective-permute-start | bytes 1572872 | tf_op jit(solution)/shard_map/ppermute | solution.py:170
  33.6 1.6 %collective-permute-done = bf16[1,8,64,256]{3,2,1,0:T(8,128)(2,1)S(1)} collective-permute-done((bf16[1,8,64,256]{3,2,1,0:T(8,128)(2,1)S(1)}, bf16[1,8,64,256]{3,2,1,0:T(8,128)(2,1)S(1)}, u32[]{:S(2)}, u32[]{:S(2)}) %collective-permute-start) | collective-permute-done | bytes 262176 | tf_op jit(solution)/shard_map/ppermute | solution.py:170
  35.3 0.1 pad_maximum_fusion.rest_0_
  35.3 1.3 %collective-permute-start.1 = (bf16[2,8,64,256]{3,2,1,0:T(8,128)(2,1)S(1)}, bf16[2,8,64,256]{3,2,1,0:T(8,128)(2,1)}, u32[]{:S(2)}, u32[]{:S(2)}) collective-permute-start(bf16[2,8,64,256]{3,2,1,0:T(8,128)(2,1)S(1)} %pad_maximum_fusion.rest_0_), channel_id=1, source_target_pairs={{0,2},{1,9},{2,4},{3,11},{4,6},{5,13},{6,0},{7,15},{8,10},{9,17},{... | collective-permute-start | bytes 1572872 | tf_op jit(solution)/shard_map/ppermute | solution.py:170
  36.6 1.2 %collective-permute-start.9 = (bf16[2,8,64,256]{3,2,1,0:T(8,128)(2,1)S(1)}, bf16[2,8,64,256]{3,2,1,0:T(8,128)(2,1)S(1)}, u32[]{:S(2)}, u32[]{:S(2)}) collective-permute-start(bf16[2,8,64,256]{3,2,1,0:T(8,128)(2,1)S(1)} %constant_dynamic-update-slice_fusion.rest_1_), channel_id=1, source_target_pairs={{0,2},{1,9},{2,4},{3,11},{4,6},{5,13},{6,0},{7,15},{8,10},{9,17},{... | collective-permute-start | bytes 1572872 | tf_op jit(solution)/shard_map/ppermute | solution.py:170
  37.8 1.5 %collective-permute-start.10 = (bf16[2,8,64,256]{3,2,1,0:T(8,128)(2,1)S(1)}, bf16[2,8,64,256]{3,2,1,0:T(8,128)(2,1)S(1)}, u32[]{:S(2)}, u32[]{:S(2)}) collective-permute-start(bf16[2,8,64,256]{3,2,1,0:T(8,128)(2,1)S(1)} %pad_maximum_fusion.rest_0_), channel_id=1, source_target_pairs={{0,6},{1,25},{2,0},{3,27},{4,2},{5,29},{6,4},{7,31},{8,14},{9,1},{... | collective-permute-start | bytes 1572872 | tf_op jit(solution)/shard_map/ppermute | solution.py:170
  39.3 4.1 %all-to-all-done.q_ref = bf16[8,64,512]{2,1,0:T(8,128)(2,1)S(1)} async-done(((bf16[8,64,512]{2,1,0:T(8,128)(2,1)}), bf16[8,64,512]{2,1,0:T(8,128)(2,1)S(1)}, u32[]{:S(2)}, u32[]{:S(2)}) %all-to-all-start) | async-done | bytes 524320 | tf_op jit(solution)/shard_map/all_to_all | solution.py:212
  43.4 3.7 %collective-permute-start.8 = (bf16[2,8,64,256]{3,2,1,0:T(8,128)(2,1)S(1)}, bf16[2,8,64,256]{3,2,1,0:T(8,128)(2,1)S(1)}, u32[]{:S(2)}, u32[]{:S(2)}) collective-permute-start(bf16[2,8,64,256]{3,2,1,0:T(8,128)(2,1)S(1)} %constant_dynamic-update-slice_fusion.rest_1_), channel_id=1, source_target_pairs={{0,1},{1,0},{2,3},{3,2},{4,5},{5,4},{6,7},{7,6},{8,9},{9,8},{10,11... | collective-permute-start | bytes 1572872 | tf_op jit(solution)/shard_map/ppermute | solution.py:174
  47.1 0.0 collective-permute-done.5.rest_3_
  47.1 0.0 collective-permute-start.7
  47.1 0.0 collective-permute-done.1.rest_2_
  47.1 2.6 %collective-permute-start.6 = (bf16[2,8,64,256]{3,2,1,0:T(8,128)(2,1)S(1)}, bf16[2,8,64,256]{3,2,1,0:T(8,128)(2,1)S(1)}, u32[]{:S(2)}, u32[]{:S(2)}) collective-permute-start(bf16[2,8,64,256]{3,2,1,0:T(8,128)(2,1)S(1)} %collective-permute-done.5.rest_3_), channel_id=1, source_target_pairs={{0,6},{1,25},{2,0},{3,27},{4,2},{5,29},{6,4},{7,31},{8,14},{9,1},{... | collective-permute-start | bytes 1572872 | tf_op jit(solution)/shard_map/ppermute | solution.py:170
  49.7 0.1 pad_add_fusion.place_ref
  49.7 0.0 copy-done
  49.7 6.8 %shard_map.74 = (f32[8,144,256]{2,1,0:T(8,128)S(1)}, f32[8,8,256]{2,1,0:T(8,128)S(1)}) custom-call(s32[2,36]{1,0:T(2,128)S(1)} %copy-done, s32[3]{0:T(128)S(1)} %pad_add_fusion.place_ref, bf16[8,64,512]{2,1,0:T(8,128)(2,1)S(1)} %all-to-all-done.q_ref, bf16[2,8,64,256]{3,2,1,0:T(8,128)(2,1)S(1)} %pad_maximum_fusion.rest_0_, ...), custom_call_target="tpu_custom_call" | custom-call | flops 2415919104 | bytes 8388608 | tf_op jit(solution)/shard_map/pallas_call | solution.py:151
  56.6 0.0 collective-permute-done.9.rest_2_
  56.6 0.1 collective-permute-start.2
  56.7 0.0 collective-permute-done.10.rest_3_
  56.7 3.4 %collective-permute-start.13 = (bf16[2,8,64,256]{3,2,1,0:T(8,128)(2,1)}, bf16[2,8,64,256]{3,2,1,0:T(8,128)(2,1)S(1)}, u32[]{:S(2)}, u32[]{:S(2)}) collective-permute-start(bf16[2,8,64,256]{3,2,1,0:T(8,128)(2,1)} %collective-permute-done.1.rest_2_), channel_id=1, source_target_pairs={{0,1},{1,0},{2,3},{3,2},{4,5},{5,4},{6,7},{7,6},{8,9},{9,8},{10,11... | collective-permute-start | bytes 1572872 | tf_op jit(solution)/shard_map/ppermute | solution.py:174
  60.1 0.0 collective-permute-done.8.rest_1_
  60.1 0.3 collective-permute-start.14
  60.3 0.0 collective-permute-done.7.rest_0_
  60.3 0.2 collective-permute-start.15
  60.6 0.0 collective-permute-done.6.rest_1_
  60.6 0.3 collective-permute-start.16
  60.9 6.2 %shard_map.75 = (f32[8,144,256]{2,1,0:T(8,128)S(1)}, f32[8,8,256]{2,1,0:T(8,128)S(1)}) custom-call(s32[2,36]{1,0:T(2,128)S(1)} %copy-done, s32[3]{0:T(128)S(1)} %pad_add_fusion.place_ref, bf16[8,64,512]{2,1,0:T(8,128)(2,1)S(1)} %all-to-all-done.q_ref, ...), custom_call_target="tpu_custom_call", output_to_operand_aliasing={{0}: (7, {}), {1}: (8, {})} | custom-call | flops 2415919104 | bytes 8388608 | tf_op jit(solution)/shard_map/pallas_call | solution.py:151
  67.1 0.0 collective-permute-done.2.rest_0_
  67.1 3.4 %collective-permute-start.12 = (bf16[2,8,64,256]{3,2,1,0:T(8,128)(2,1)S(1)}, bf16[2,8,64,256]{3,2,1,0:T(8,128)(2,1)S(1)}, u32[]{:S(2)}, u32[]{:S(2)}) collective-permute-start(bf16[2,8,64,256]{3,2,1,0:T(8,128)(2,1)S(1)} %collective-permute-done.6.rest_1_), channel_id=1, source_target_pairs={{0,1},{1,0},{2,3},{3,2},{4,5},{5,4},{6,7},{7,6},{8,9},{9,8},{10,11... | collective-permute-start | bytes 1572872 | tf_op jit(solution)/shard_map/ppermute | solution.py:174
  70.5 0.0 collective-permute-done.13.rest_0_
  70.5 0.0 collective-permute-start.11
  70.6 0.0 collective-permute-done.14.rest_1_
  70.6 0.0 collective-permute-done.15.rest_2_
  70.6 0.0 collective-permute-done.16.rest_3_
  70.6 6.3 %shard_map.76 = (f32[8,144,256]{2,1,0:T(8,128)S(1)}, f32[8,8,256]{2,1,0:T(8,128)S(1)}) custom-call(s32[2,36]{1,0:T(2,128)S(1)} %copy-done, s32[3]{0:T(128)S(1)} %pad_add_fusion.place_ref, bf16[8,64,512]{2,1,0:T(8,128)(2,1)S(1)} %all-to-all-done.q_ref, ...), custom_call_target="tpu_custom_call", output_to_operand_aliasing={{0}: (7, {}), {1}: (8, {})} | custom-call | flops 2415919104 | bytes 8388608 | tf_op jit(solution)/shard_map/pallas_call | solution.py:151
  76.9 0.0 collective-permute-done.12.rest_3_
  76.9 0.0 collective-permute-done.11.rest_2_
  76.9 6.5 %shard_map.77 = bf16[8,64,512]{2,1,0:T(8,128)(2,1)S(1)} custom-call(s32[2,36]{1,0:T(2,128)S(1)} %copy-done, s32[3]{0:T(128)S(1)} %pad_add_fusion.place_ref, bf16[8,64,512]{2,1,0:T(8,128)(2,1)S(1)} %all-to-all-done.q_ref, bf16[2,8,64,256]{3,2,1,0:T(8,128)(2,1)S(1)} %collective-permute-done.2.rest_0_, ...), custom_call_target="tpu_custom_call" | custom-call | flops 2415919104 | bytes 8388608 | tf_op jit(solution)/shard_map/pallas_call | solution.py:151
  83.4 23.8 %all_to_all.16 = bf16[8,64,512]{2,1,0:T(8,128)(2,1)S(1)} all-to-all(bf16[8,64,512]{2,1,0:T(8,128)(2,1)S(1)} %shard_map.77), channel_id=1, replica_groups=mesh['z'=8,'x'=4,'y'=4,'c'=2] {'z'}, dimensions={0} | all-to-all | bytes 1048576 | tf_op jit(solution)/shard_map/all_to_all | solution.py:259
  107.2 0.8 copy.15
  (2 shorter events, 0.0 us)
Async XLA Ops:
  0.0 24.4 %copy-start.1 = (bf16[64,4096]{1,0:T(8,128)(2,1)S(1)}, bf16[64,4096]{1,0:T(8,128)(2,1)}, u32[]{:S(2)}) copy-start(bf16[64,4096]{1,0:T(8,128)(2,1)} %param.7) | copy-start | bytes 1572868
  21.3 8.9 %collective-permute-start.3 = (bf16[1,8,64,256]{3,2,1,0:T(8,128)(2,1)S(1)}, bf16[1,8,64,256]{3,2,1,0:T(8,128)(2,1)S(1)}, u32[]{:S(2)}, u32[]{:S(2)}) collective-permute-start(bf16[1,8,64,256]{3,2,1,0:T(8,128)(2,1)S(1)} %bitcast.15), channel_id=1, source_target_pairs={{0,24},{1,7},{2,26},{3,1},{4,28},{5,3},{6,30},{7,5},{8,0},{9,15},{... | collective-permute-start | bytes 786440 | tf_op jit(solution)/shard_map/ppermute | solution.py:170
  24.0 6.7 %collective-permute-start.4 = (bf16[1,8,64,256]{3,2,1,0:T(8,128)(2,1)S(1)}, bf16[1,8,64,256]{3,2,1,0:T(8,128)(2,1)S(1)}, u32[]{:S(2)}, u32[]{:S(2)}) collective-permute-start(bf16[1,8,64,256]{3,2,1,0:T(8,128)(2,1)S(1)} %bitcast.16), channel_id=1, source_target_pairs={{0,16},{1,5},{2,18},{3,7},{4,20},{5,1},{6,22},{7,3},{8,24},{9,13},... | collective-permute-start | bytes 786440 | tf_op jit(solution)/shard_map/ppermute | solution.py:170
  25.2 18.1 %all-to-all-start = ((bf16[8,64,512]{2,1,0:T(8,128)(2,1)}), bf16[8,64,512]{2,1,0:T(8,128)(2,1)S(1)}, u32[]{:S(2)}, u32[]{:S(2)}) async-start(bf16[8,64,512]{2,1,0:T(8,128)(2,1)} %bitcast.13), calls=%async_computation | async-start | bytes 1048576 | tf_op jit(solution)/shard_map/all_to_all | solution.py:212
  28.7 21.0 %copy-start = (s32[2,36]{1,0:T(2,128)S(1)}, s32[2,36]{1,0:T(2,128)}, u32[]{:S(2)}) copy-start(s32[2,36]{1,0:T(2,128)} %constant.13.clone.table_ref) | copy-start | bytes 868
  28.7 6.5 %collective-permute-start = (bf16[1,8,64,256]{3,2,1,0:T(8,128)(2,1)S(1)}, bf16[1,8,64,256]{3,2,1,0:T(8,128)(2,1)S(1)}, u32[]{:S(2)}, u32[]{:S(2)}) collective-permute-start(bf16[1,8,64,256]{3,2,1,0:T(8,128)(2,1)S(1)} %bitcast.17), channel_id=1, source_target_pairs={{0,8},{1,3},{2,10},{3,5},{4,12},{5,7},{6,14},{7,1},{8,16},{9,11},{... | collective-permute-start | bytes 786440 | tf_op jit(solution)/shard_map/ppermute | solution.py:170
  30.8 16.3 %collective-permute-start.5 = (bf16[2,8,64,256]{3,2,1,0:T(8,128)(2,1)S(1)}, bf16[2,8,64,256]{3,2,1,0:T(8,128)(2,1)S(1)}, u32[]{:S(2)}, u32[]{:S(2)}) collective-permute-start(bf16[2,8,64,256]{3,2,1,0:T(8,128)(2,1)S(1)} %constant_dynamic-update-slice_fusion.rest_1_), channel_id=1, source_target_pairs={{0,6},{1,25},{2,0},{3,27},{4,2},{5,29},{6,4},{7,31},{8,14},{9,1},{... | collective-permute-start | bytes 1572872 | tf_op jit(solution)/shard_map/ppermute | solution.py:170
  35.3 11.8 %collective-permute-start.1 = (bf16[2,8,64,256]{3,2,1,0:T(8,128)(2,1)S(1)}, bf16[2,8,64,256]{3,2,1,0:T(8,128)(2,1)}, u32[]{:S(2)}, u32[]{:S(2)}) collective-permute-start(bf16[2,8,64,256]{3,2,1,0:T(8,128)(2,1)S(1)} %pad_maximum_fusion.rest_0_), channel_id=1, source_target_pairs={{0,2},{1,9},{2,4},{3,11},{4,6},{5,13},{6,0},{7,15},{8,10},{9,17},{... | collective-permute-start | bytes 1572872 | tf_op jit(solution)/shard_map/ppermute | solution.py:170
  36.6 20.0 %collective-permute-start.9 = (bf16[2,8,64,256]{3,2,1,0:T(8,128)(2,1)S(1)}, bf16[2,8,64,256]{3,2,1,0:T(8,128)(2,1)S(1)}, u32[]{:S(2)}, u32[]{:S(2)}) collective-permute-start(bf16[2,8,64,256]{3,2,1,0:T(8,128)(2,1)S(1)} %constant_dynamic-update-slice_fusion.rest_1_), channel_id=1, source_target_pairs={{0,2},{1,9},{2,4},{3,11},{4,6},{5,13},{6,0},{7,15},{8,10},{9,17},{... | collective-permute-start | bytes 1572872 | tf_op jit(solution)/shard_map/ppermute | solution.py:170
  37.8 18.8 %collective-permute-start.10 = (bf16[2,8,64,256]{3,2,1,0:T(8,128)(2,1)S(1)}, bf16[2,8,64,256]{3,2,1,0:T(8,128)(2,1)S(1)}, u32[]{:S(2)}, u32[]{:S(2)}) collective-permute-start(bf16[2,8,64,256]{3,2,1,0:T(8,128)(2,1)S(1)} %pad_maximum_fusion.rest_0_), channel_id=1, source_target_pairs={{0,6},{1,25},{2,0},{3,27},{4,2},{5,29},{6,4},{7,31},{8,14},{9,1},{... | collective-permute-start | bytes 1572872 | tf_op jit(solution)/shard_map/ppermute | solution.py:170
  43.4 16.7 %collective-permute-start.8 = (bf16[2,8,64,256]{3,2,1,0:T(8,128)(2,1)S(1)}, bf16[2,8,64,256]{3,2,1,0:T(8,128)(2,1)S(1)}, u32[]{:S(2)}, u32[]{:S(2)}) collective-permute-start(bf16[2,8,64,256]{3,2,1,0:T(8,128)(2,1)S(1)} %constant_dynamic-update-slice_fusion.rest_1_), channel_id=1, source_target_pairs={{0,1},{1,0},{2,3},{3,2},{4,5},{5,4},{6,7},{7,6},{8,9},{9,8},{10,11... | collective-permute-start | bytes 1572872 | tf_op jit(solution)/shard_map/ppermute | solution.py:174
  47.1 13.3 %collective-permute-start.7 = (bf16[2,8,64,256]{3,2,1,0:T(8,128)(2,1)S(1)}, bf16[2,8,64,256]{3,2,1,0:T(8,128)(2,1)S(1)}, u32[]{:S(2)}, u32[]{:S(2)}) collective-permute-start(bf16[2,8,64,256]{3,2,1,0:T(8,128)(2,1)S(1)} %pad_maximum_fusion.rest_0_), channel_id=1, source_target_pairs={{0,1},{1,0},{2,3},{3,2},{4,5},{5,4},{6,7},{7,6},{8,9},{9,8},{10,11... | collective-permute-start | bytes 1572872 | tf_op jit(solution)/shard_map/ppermute | solution.py:174
  47.1 13.5 %collective-permute-start.6 = (bf16[2,8,64,256]{3,2,1,0:T(8,128)(2,1)S(1)}, bf16[2,8,64,256]{3,2,1,0:T(8,128)(2,1)S(1)}, u32[]{:S(2)}, u32[]{:S(2)}) collective-permute-start(bf16[2,8,64,256]{3,2,1,0:T(8,128)(2,1)S(1)} %collective-permute-done.5.rest_3_), channel_id=1, source_target_pairs={{0,6},{1,25},{2,0},{3,27},{4,2},{5,29},{6,4},{7,31},{8,14},{9,1},{... | collective-permute-start | bytes 1572872 | tf_op jit(solution)/shard_map/ppermute | solution.py:170
  56.6 10.5 %collective-permute-start.2 = (bf16[2,8,64,256]{3,2,1,0:T(8,128)(2,1)}, bf16[2,8,64,256]{3,2,1,0:T(8,128)(2,1)S(1)}, u32[]{:S(2)}, u32[]{:S(2)}) collective-permute-start(bf16[2,8,64,256]{3,2,1,0:T(8,128)(2,1)} %collective-permute-done.1.rest_2_), channel_id=1, source_target_pairs={{0,2},{1,9},{2,4},{3,11},{4,6},{5,13},{6,0},{7,15},{8,10},{9,17},{... | collective-permute-start | bytes 1572872 | tf_op jit(solution)/shard_map/ppermute | solution.py:170
  56.7 13.9 %collective-permute-start.13 = (bf16[2,8,64,256]{3,2,1,0:T(8,128)(2,1)}, bf16[2,8,64,256]{3,2,1,0:T(8,128)(2,1)S(1)}, u32[]{:S(2)}, u32[]{:S(2)}) collective-permute-start(bf16[2,8,64,256]{3,2,1,0:T(8,128)(2,1)} %collective-permute-done.1.rest_2_), channel_id=1, source_target_pairs={{0,1},{1,0},{2,3},{3,2},{4,5},{5,4},{6,7},{7,6},{8,9},{9,8},{10,11... | collective-permute-start | bytes 1572872 | tf_op jit(solution)/shard_map/ppermute | solution.py:174
  60.1 10.5 %collective-permute-start.14 = (bf16[2,8,64,256]{3,2,1,0:T(8,128)(2,1)S(1)}, bf16[2,8,64,256]{3,2,1,0:T(8,128)(2,1)S(1)}, u32[]{:S(2)}, u32[]{:S(2)}) collective-permute-start(bf16[2,8,64,256]{3,2,1,0:T(8,128)(2,1)S(1)} %collective-permute-done.5.rest_3_), channel_id=1, source_target_pairs={{0,1},{1,0},{2,3},{3,2},{4,5},{5,4},{6,7},{7,6},{8,9},{9,8},{10,11... | collective-permute-start | bytes 1572872 | tf_op jit(solution)/shard_map/ppermute | solution.py:174
  60.3 10.2 %collective-permute-start.15 = (bf16[2,8,64,256]{3,2,1,0:T(8,128)(2,1)S(1)}, bf16[2,8,64,256]{3,2,1,0:T(8,128)(2,1)S(1)}, u32[]{:S(2)}, u32[]{:S(2)}) collective-permute-start(bf16[2,8,64,256]{3,2,1,0:T(8,128)(2,1)S(1)} %collective-permute-done.9.rest_2_), channel_id=1, source_target_pairs={{0,1},{1,0},{2,3},{3,2},{4,5},{5,4},{6,7},{7,6},{8,9},{9,8},{10,11... | collective-permute-start | bytes 1572872 | tf_op jit(solution)/shard_map/ppermute | solution.py:174
  60.6 10.0 %collective-permute-start.16 = (bf16[2,8,64,256]{3,2,1,0:T(8,128)(2,1)S(1)}, bf16[2,8,64,256]{3,2,1,0:T(8,128)(2,1)S(1)}, u32[]{:S(2)}, u32[]{:S(2)}) collective-permute-start(bf16[2,8,64,256]{3,2,1,0:T(8,128)(2,1)S(1)} %collective-permute-done.10.rest_3_), channel_id=1, source_target_pairs={{0,1},{1,0},{2,3},{3,2},{4,5},{5,4},{6,7},{7,6},{8,9},{9,8},{10,11... | collective-permute-start | bytes 1572872 | tf_op jit(solution)/shard_map/ppermute | solution.py:174
  67.1 9.7 %collective-permute-start.12 = (bf16[2,8,64,256]{3,2,1,0:T(8,128)(2,1)S(1)}, bf16[2,8,64,256]{3,2,1,0:T(8,128)(2,1)S(1)}, u32[]{:S(2)}, u32[]{:S(2)}) collective-permute-start(bf16[2,8,64,256]{3,2,1,0:T(8,128)(2,1)S(1)} %collective-permute-done.6.rest_1_), channel_id=1, source_target_pairs={{0,1},{1,0},{2,3},{3,2},{4,5},{5,4},{6,7},{7,6},{8,9},{9,8},{10,11... | collective-permute-start | bytes 1572872 | tf_op jit(solution)/shard_map/ppermute | solution.py:174
  70.5 6.3 %collective-permute-start.11 = (bf16[2,8,64,256]{3,2,1,0:T(8,128)(2,1)S(1)}, bf16[2,8,64,256]{3,2,1,0:T(8,128)(2,1)S(1)}, u32[]{:S(2)}, u32[]{:S(2)}) collective-permute-start(bf16[2,8,64,256]{3,2,1,0:T(8,128)(2,1)S(1)} %collective-permute-done.2.rest_0_), channel_id=1, source_target_pairs={{0,1},{1,0},{2,3},{3,2},{4,5},{5,4},{6,7},{7,6},{8,9},{9,8},{10,11... | collective-permute-start | bytes 1572872 | tf_op jit(solution)/shard_map/ppermute | solution.py:174

commit v3 on v2

--- a/solution.py
+++ b/solution.py
@@ -27,7 +27,7 @@
         _used[s] += 1
 assert _used == list(range(SPANS))
 WIDE = 4
-EXTRA = 16
+EXTRA = 8
 
 
 def turn_kernel(table_ref, place_ref, q_ref, *rest, kinds, first, last):
@@ -123,7 +123,8 @@
     both(None, (count - 1, 0))
     if last:
         for tile in range(SPANS):
-            mixed = (acc_ref[tile, pl.ds(0, HEAD_DIM)] / acc_ref[tile, pl.ds(HEAD_DIM, 1)]).T.astype(jnp.bfloat16)
+            share = 1.0 / acc_ref[tile, pl.ds(HEAD_DIM, 1)]
+            mixed = (acc_ref[tile, pl.ds(0, HEAD_DIM)] * share).T.astype(jnp.bfloat16)
             for h in range(GROUP):
                 out_ref[tile, :, pl.ds(h * HEAD_DIM, HEAD_DIM)] = mixed[h * toks : (h + 1) * toks]
 

time: 108 us -> 108 us (level)
  no operation moved by 1% of the time
where the time goes in v3:
time: 108 us
  blocking collectives  43.3 us (40%)
  starting transfers between devices  28.1 us (26%)
  Pallas kernels  27.5 us (25%)
  waiting for transfers between devices  6.98 us (6%)
  local copies, waits for them, and re-layouts  1.72 us (2%)
    pallas_call x4, Pallas kernels, turn(): pl.pallas_call(functools.partial(turn_kernel, kinds=kinds, first=first, l...  25.8 us
    all_to_all x1, blocking collectives, per_device(): out = lax.all_to_all(out, 'z', 0, 0, tiled=True)  23.8 us
    all_to_all x1, blocking collectives, per_device(): kv = lax.all_to_all(kv, 'z', 0, 0, tiled=True)[None]  19.5 us
    ppermute x9, starting transfers between devices, hop(): return lax.ppermute(value, PLANE, pairs)  13.3 us
    ppermute x8, starting transfers between devices, swap(): return lax.ppermute(value, 'c', [(0, 1), (1, 0)])  11.3 us
    all_to_all x1, waiting for transfers between devices, per_device(): q = lax.all_to_all(q, 'z', 0, 0, tiled=True)  4.1 us
    all_to_all x1, starting transfers between devices, per_device(): q = lax.all_to_all(q, 'z', 0, 0, tiled=True)  3.49 us
    ppermute x9, waiting for transfers between devices, hop(): return lax.ppermute(value, PLANE, pairs)  2.86 us
  transfers between devices with their start and end apart: 18, of which 4 were waited for; matrix products, arithmetic and copies ran while one was open for 1% of the time, Pallas kernels for 18%

profile of v3, /device:TPU:1, one launch (start us, length us, event | category | flops | bytes accessed | tf_op | source)
XLA Modules:
  0.0 108.0 jit_solution(1624613952343580952)
XLA Ops:
  0.0 0.0 copy-start.1
  0.0 1.8 %shard_map.73 = bf16[8,64,256]{2,1,0:T(8,128)(2,1)} custom-call(bf16[64,1024]{1,0:T(8,128)(2,1)} %key_ref.1, bf16[64,1024]{1,0:T(8,128)(2,1)} %value_ref.1), custom_call_target="tpu_custom_call" | custom-call | tf_op jit(solution)/shard_map/pallas_call | solution.py:193
  1.8 19.5 %all_to_all.15 = bf16[8,64,256]{2,1,0:T(8,128)(2,1)S(1)} all-to-all(bf16[8,64,256]{2,1,0:T(8,128)(2,1)} %shard_map.73), channel_id=1, replica_groups=mesh['z'=8,'x'=4,'y'=4,'c'=2] {'z'}, dimensions={0} | all-to-all | bytes 524288 | tf_op jit(solution)/shard_map/all_to_all | solution.py:211
  21.3 2.7 %collective-permute-start.3 = (bf16[1,8,64,256]{3,2,1,0:T(8,128)(2,1)S(1)}, bf16[1,8,64,256]{3,2,1,0:T(8,128)(2,1)S(1)}, u32[]{:S(2)}, u32[]{:S(2)}) collective-permute-start(bf16[1,8,64,256]{3,2,1,0:T(8,128)(2,1)S(1)} %bitcast.15), channel_id=1, source_target_pairs={{0,24},{1,7},{2,26},{3,1},{4,28},{5,3},{6,30},{7,5},{8,0},{9,15},{... | collective-permute-start | bytes 786440 | tf_op jit(solution)/shard_map/ppermute | solution.py:171
  24.0 0.3 collective-permute-start.4
  24.4 0.0 copy-done.1
  24.4 0.8 copy.17
  25.2 3.5 %all-to-all-start = ((bf16[8,64,512]{2,1,0:T(8,128)(2,1)}), bf16[8,64,512]{2,1,0:T(8,128)(2,1)S(1)}, u32[]{:S(2)}, u32[]{:S(2)}) async-start(bf16[8,64,512]{2,1,0:T(8,128)(2,1)} %bitcast.13), calls=%async_computation | async-start | bytes 1048576 | tf_op jit(solution)/shard_map/all_to_all | solution.py:213
  28.7 0.0 copy-start
  28.7 0.8 collective-permute-start
  29.5 0.6 collective-permute-done.3
  30.2 0.6 collective-permute-done.4
  30.8 2.9 %collective-permute-start.5 = (bf16[2,8,64,256]{3,2,1,0:T(8,128)(2,1)S(1)}, bf16[2,8,64,256]{3,2,1,0:T(8,128)(2,1)S(1)}, u32[]{:S(2)}, u32[]{:S(2)}) collective-permute-start(bf16[2,8,64,256]{3,2,1,0:T(8,128)(2,1)S(1)} %constant_dynamic-update-slice_fusion.rest_1_), channel_id=1, source_target_pairs={{0,6},{1,25},{2,0},{3,27},{4,2},{5,29},{6,4},{7,31},{8,14},{9,1},{... | collective-permute-start | bytes 1572872 | tf_op jit(solution)/shard_map/ppermute | solution.py:171
  33.6 1.6 %collective-permute-done = bf16[1,8,64,256]{3,2,1,0:T(8,128)(2,1)S(1)} collective-permute-done((bf16[1,8,64,256]{3,2,1,0:T(8,128)(2,1)S(1)}, bf16[1,8,64,256]{3,2,1,0:T(8,128)(2,1)S(1)}, u32[]{:S(2)}, u32[]{:S(2)}) %collective-permute-start) | collective-permute-done | bytes 262176 | tf_op jit(solution)/shard_map/ppermute | solution.py:171
  35.3 0.1 pad_maximum_fusion.rest_0_
  35.3 1.3 %collective-permute-start.1 = (bf16[2,8,64,256]{3,2,1,0:T(8,128)(2,1)S(1)}, bf16[2,8,64,256]{3,2,1,0:T(8,128)(2,1)}, u32[]{:S(2)}, u32[]{:S(2)}) collective-permute-start(bf16[2,8,64,256]{3,2,1,0:T(8,128)(2,1)S(1)} %pad_maximum_fusion.rest_0_), channel_id=1, source_target_pairs={{0,2},{1,9},{2,4},{3,11},{4,6},{5,13},{6,0},{7,15},{8,10},{9,17},{... | collective-permute-start | bytes 1572872 | tf_op jit(solution)/shard_map/ppermute | solution.py:171
  36.6 1.2 %collective-permute-start.9 = (bf16[2,8,64,256]{3,2,1,0:T(8,128)(2,1)S(1)}, bf16[2,8,64,256]{3,2,1,0:T(8,128)(2,1)S(1)}, u32[]{:S(2)}, u32[]{:S(2)}) collective-permute-start(bf16[2,8,64,256]{3,2,1,0:T(8,128)(2,1)S(1)} %constant_dynamic-update-slice_fusion.rest_1_), channel_id=1, source_target_pairs={{0,2},{1,9},{2,4},{3,11},{4,6},{5,13},{6,0},{7,15},{8,10},{9,17},{... | collective-permute-start | bytes 1572872 | tf_op jit(solution)/shard_map/ppermute | solution.py:171
  37.8 1.5 %collective-permute-start.10 = (bf16[2,8,64,256]{3,2,1,0:T(8,128)(2,1)S(1)}, bf16[2,8,64,256]{3,2,1,0:T(8,128)(2,1)S(1)}, u32[]{:S(2)}, u32[]{:S(2)}) collective-permute-start(bf16[2,8,64,256]{3,2,1,0:T(8,128)(2,1)S(1)} %pad_maximum_fusion.rest_0_), channel_id=1, source_target_pairs={{0,6},{1,25},{2,0},{3,27},{4,2},{5,29},{6,4},{7,31},{8,14},{9,1},{... | collective-permute-start | bytes 1572872 | tf_op jit(solution)/shard_map/ppermute | solution.py:171
  39.3 4.1 %all-to-all-done.q_ref = bf16[8,64,512]{2,1,0:T(8,128)(2,1)S(1)} async-done(((bf16[8,64,512]{2,1,0:T(8,128)(2,1)}), bf16[8,64,512]{2,1,0:T(8,128)(2,1)S(1)}, u32[]{:S(2)}, u32[]{:S(2)}) %all-to-all-start) | async-done | bytes 524320 | tf_op jit(solution)/shard_map/all_to_all | solution.py:213
  43.4 3.7 %collective-permute-start.8 = (bf16[2,8,64,256]{3,2,1,0:T(8,128)(2,1)S(1)}, bf16[2,8,64,256]{3,2,1,0:T(8,128)(2,1)S(1)}, u32[]{:S(2)}, u32[]{:S(2)}) collective-permute-start(bf16[2,8,64,256]{3,2,1,0:T(8,128)(2,1)S(1)} %constant_dynamic-update-slice_fusion.rest_1_), channel_id=1, source_target_pairs={{0,1},{1,0},{2,3},{3,2},{4,5},{5,4},{6,7},{7,6},{8,9},{9,8},{10,11... | collective-permute-start | bytes 1572872 | tf_op jit(solution)/shard_map/ppermute | solution.py:175
  47.1 0.0 collective-permute-done.5.rest_3_
  47.1 0.0 collective-permute-start.7
  47.1 0.0 collective-permute-done.1.rest_2_
  47.1 2.6 %collective-permute-start.6 = (bf16[2,8,64,256]{3,2,1,0:T(8,128)(2,1)S(1)}, bf16[2,8,64,256]{3,2,1,0:T(8,128)(2,1)S(1)}, u32[]{:S(2)}, u32[]{:S(2)}) collective-permute-start(bf16[2,8,64,256]{3,2,1,0:T(8,128)(2,1)S(1)} %collective-permute-done.5.rest_3_), channel_id=1, source_target_pairs={{0,6},{1,25},{2,0},{3,27},{4,2},{5,29},{6,4},{7,31},{8,14},{9,1},{... | collective-permute-start | bytes 1572872 | tf_op jit(solution)/shard_map/ppermute | solution.py:171
  49.7 0.1 pad_add_fusion.place_ref
  49.7 0.0 copy-done
  49.7 6.8 %shard_map.74 = (f32[8,136,256]{2,1,0:T(8,128)S(1)}, f32[8,8,256]{2,1,0:T(8,128)S(1)}) custom-call(s32[2,36]{1,0:T(2,128)S(1)} %copy-done, s32[3]{0:T(128)S(1)} %pad_add_fusion.place_ref, bf16[8,64,512]{2,1,0:T(8,128)(2,1)S(1)} %all-to-all-done.q_ref, bf16[2,8,64,256]{3,2,1,0:T(8,128)(2,1)S(1)} %pad_maximum_fusion.rest_0_, ...), custom_call_target="tpu_custom_call" | custom-call | flops 2415919104 | bytes 8388608 | tf_op jit(solution)/shard_map/pallas_call | solution.py:152
  56.5 0.0 collective-permute-done.9.rest_2_
  56.5 0.1 collective-permute-start.2
  56.6 0.0 collective-permute-done.10.rest_3_
  56.6 3.4 %collective-permute-start.13 = (bf16[2,8,64,256]{3,2,1,0:T(8,128)(2,1)}, bf16[2,8,64,256]{3,2,1,0:T(8,128)(2,1)S(1)}, u32[]{:S(2)}, u32[]{:S(2)}) collective-permute-start(bf16[2,8,64,256]{3,2,1,0:T(8,128)(2,1)} %collective-permute-done.1.rest_2_), channel_id=1, source_target_pairs={{0,1},{1,0},{2,3},{3,2},{4,5},{5,4},{6,7},{7,6},{8,9},{9,8},{10,11... | collective-permute-start | bytes 1572872 | tf_op jit(solution)/shard_map/ppermute | solution.py:175
  60.0 0.0 collective-permute-done.8.rest_1_
  60.0 0.3 collective-permute-start.14
  60.3 0.0 collective-permute-done.7.rest_0_
  60.3 0.2 collective-permute-start.15
  60.5 0.0 collective-permute-done.6.rest_1_
  60.5 0.3 collective-permute-start.16
  60.8 6.2 %shard_map.75 = (f32[8,136,256]{2,1,0:T(8,128)S(1)}, f32[8,8,256]{2,1,0:T(8,128)S(1)}) custom-call(s32[2,36]{1,0:T(2,128)S(1)} %copy-done, s32[3]{0:T(128)S(1)} %pad_add_fusion.place_ref, bf16[8,64,512]{2,1,0:T(8,128)(2,1)S(1)} %all-to-all-done.q_ref, ...), custom_call_target="tpu_custom_call", output_to_operand_aliasing={{0}: (7, {}), {1}: (8, {})} | custom-call | flops 2415919104 | bytes 8388608 | tf_op jit(solution)/shard_map/pallas_call | solution.py:152
  67.1 0.0 collective-permute-done.2.rest_0_
  67.1 3.4 %collective-permute-start.12 = (bf16[2,8,64,256]{3,2,1,0:T(8,128)(2,1)S(1)}, bf16[2,8,64,256]{3,2,1,0:T(8,128)(2,1)S(1)}, u32[]{:S(2)}, u32[]{:S(2)}) collective-permute-start(bf16[2,8,64,256]{3,2,1,0:T(8,128)(2,1)S(1)} %collective-permute-done.6.rest_1_), channel_id=1, source_target_pairs={{0,1},{1,0},{2,3},{3,2},{4,5},{5,4},{6,7},{7,6},{8,9},{9,8},{10,11... | collective-permute-start | bytes 1572872 | tf_op jit(solution)/shard_map/ppermute | solution.py:175
  70.5 0.0 collective-permute-done.13.rest_0_
  70.5 0.0 collective-permute-start.11
  70.5 0.0 collective-permute-done.14.rest_1_
  70.5 0.0 collective-permute-done.15.rest_2_
  70.5 0.0 collective-permute-done.16.rest_3_
  70.5 6.3 %shard_map.76 = (f32[8,136,256]{2,1,0:T(8,128)S(1)}, f32[8,8,256]{2,1,0:T(8,128)S(1)}) custom-call(s32[2,36]{1,0:T(2,128)S(1)} %copy-done, s32[3]{0:T(128)S(1)} %pad_add_fusion.place_ref, bf16[8,64,512]{2,1,0:T(8,128)(2,1)S(1)} %all-to-all-done.q_ref, ...), custom_call_target="tpu_custom_call", output_to_operand_aliasing={{0}: (7, {}), {1}: (8, {})} | custom-call | flops 2415919104 | bytes 8388608 | tf_op jit(solution)/shard_map/pallas_call | solution.py:152
  76.8 0.0 collective-permute-done.12.rest_3_
  76.8 0.0 collective-permute-done.11.rest_2_
  76.8 6.5 %shard_map.77 = bf16[8,64,512]{2,1,0:T(8,128)(2,1)S(1)} custom-call(s32[2,36]{1,0:T(2,128)S(1)} %copy-done, s32[3]{0:T(128)S(1)} %pad_add_fusion.place_ref, bf16[8,64,512]{2,1,0:T(8,128)(2,1)S(1)} %all-to-all-done.q_ref, bf16[2,8,64,256]{3,2,1,0:T(8,128)(2,1)S(1)} %collective-permute-done.2.rest_0_, ...), custom_call_target="tpu_custom_call" | custom-call | flops 2415919104 | bytes 8388608 | tf_op jit(solution)/shard_map/pallas_call | solution.py:152
  83.3 23.8 %all_to_all.16 = bf16[8,64,512]{2,1,0:T(8,128)(2,1)S(1)} all-to-all(bf16[8,64,512]{2,1,0:T(8,128)(2,1)S(1)} %shard_map.77), channel_id=1, replica_groups=mesh['z'=8,'x'=4,'y'=4,'c'=2] {'z'}, dimensions={0} | all-to-all | bytes 1048576 | tf_op jit(solution)/shard_map/all_to_all | solution.py:260
  107.1 0.8 copy.15
  (2 shorter events, 0.0 us)
Async XLA Ops:
  0.0 24.4 %copy-start.1 = (bf16[64,4096]{1,0:T(8,128)(2,1)S(1)}, bf16[64,4096]{1,0:T(8,128)(2,1)}, u32[]{:S(2)}) copy-start(bf16[64,4096]{1,0:T(8,128)(2,1)} %param.7) | copy-start | bytes 1572868
  21.3 8.9 %collective-permute-start.3 = (bf16[1,8,64,256]{3,2,1,0:T(8,128)(2,1)S(1)}, bf16[1,8,64,256]{3,2,1,0:T(8,128)(2,1)S(1)}, u32[]{:S(2)}, u32[]{:S(2)}) collective-permute-start(bf16[1,8,64,256]{3,2,1,0:T(8,128)(2,1)S(1)} %bitcast.15), channel_id=1, source_target_pairs={{0,24},{1,7},{2,26},{3,1},{4,28},{5,3},{6,30},{7,5},{8,0},{9,15},{... | collective-permute-start | bytes 786440 | tf_op jit(solution)/shard_map/ppermute | solution.py:171
  24.0 6.7 %collective-permute-start.4 = (bf16[1,8,64,256]{3,2,1,0:T(8,128)(2,1)S(1)}, bf16[1,8,64,256]{3,2,1,0:T(8,128)(2,1)S(1)}, u32[]{:S(2)}, u32[]{:S(2)}) collective-permute-start(bf16[1,8,64,256]{3,2,1,0:T(8,128)(2,1)S(1)} %bitcast.16), channel_id=1, source_target_pairs={{0,16},{1,5},{2,18},{3,7},{4,20},{5,1},{6,22},{7,3},{8,24},{9,13},... | collective-permute-start | bytes 786440 | tf_op jit(solution)/shard_map/ppermute | solution.py:171
  25.2 18.1 %all-to-all-start = ((bf16[8,64,512]{2,1,0:T(8,128)(2,1)}), bf16[8,64,512]{2,1,0:T(8,128)(2,1)S(1)}, u32[]{:S(2)}, u32[]{:S(2)}) async-start(bf16[8,64,512]{2,1,0:T(8,128)(2,1)} %bitcast.13), calls=%async_computation | async-start | bytes 1048576 | tf_op jit(solution)/shard_map/all_to_all | solution.py:213
  28.7 21.0 %copy-start = (s32[2,36]{1,0:T(2,128)S(1)}, s32[2,36]{1,0:T(2,128)}, u32[]{:S(2)}) copy-start(s32[2,36]{1,0:T(2,128)} %constant.13.clone.table_ref) | copy-start | bytes 868
  28.7 6.5 %collective-permute-start = (bf16[1,8,64,256]{3,2,1,0:T(8,128)(2,1)S(1)}, bf16[1,8,64,256]{3,2,1,0:T(8,128)(2,1)S(1)}, u32[]{:S(2)}, u32[]{:S(2)}) collective-permute-start(bf16[1,8,64,256]{3,2,1,0:T(8,128)(2,1)S(1)} %bitcast.17), channel_id=1, source_target_pairs={{0,8},{1,3},{2,10},{3,5},{4,12},{5,7},{6,14},{7,1},{8,16},{9,11},{... | collective-permute-start | bytes 786440 | tf_op jit(solution)/shard_map/ppermute | solution.py:171
  30.8 16.3 %collective-permute-start.5 = (bf16[2,8,64,256]{3,2,1,0:T(8,128)(2,1)S(1)}, bf16[2,8,64,256]{3,2,1,0:T(8,128)(2,1)S(1)}, u32[]{:S(2)}, u32[]{:S(2)}) collective-permute-start(bf16[2,8,64,256]{3,2,1,0:T(8,128)(2,1)S(1)} %constant_dynamic-update-slice_fusion.rest_1_), channel_id=1, source_target_pairs={{0,6},{1,25},{2,0},{3,27},{4,2},{5,29},{6,4},{7,31},{8,14},{9,1},{... | collective-permute-start | bytes 1572872 | tf_op jit(solution)/shard_map/ppermute | solution.py:171
  35.3 11.8 %collective-permute-start.1 = (bf16[2,8,64,256]{3,2,1,0:T(8,128)(2,1)S(1)}, bf16[2,8,64,256]{3,2,1,0:T(8,128)(2,1)}, u32[]{:S(2)}, u32[]{:S(2)}) collective-permute-start(bf16[2,8,64,256]{3,2,1,0:T(8,128)(2,1)S(1)} %pad_maximum_fusion.rest_0_), channel_id=1, source_target_pairs={{0,2},{1,9},{2,4},{3,11},{4,6},{5,13},{6,0},{7,15},{8,10},{9,17},{... | collective-permute-start | bytes 1572872 | tf_op jit(solution)/shard_map/ppermute | solution.py:171
  36.6 19.9 %collective-permute-start.9 = (bf16[2,8,64,256]{3,2,1,0:T(8,128)(2,1)S(1)}, bf16[2,8,64,256]{3,2,1,0:T(8,128)(2,1)S(1)}, u32[]{:S(2)}, u32[]{:S(2)}) collective-permute-start(bf16[2,8,64,256]{3,2,1,0:T(8,128)(2,1)S(1)} %constant_dynamic-update-slice_fusion.rest_1_), channel_id=1, source_target_pairs={{0,2},{1,9},{2,4},{3,11},{4,6},{5,13},{6,0},{7,15},{8,10},{9,17},{... | collective-permute-start | bytes 1572872 | tf_op jit(solution)/shard_map/ppermute | solution.py:171
  37.8 18.8 %collective-permute-start.10 = (bf16[2,8,64,256]{3,2,1,0:T(8,128)(2,1)S(1)}, bf16[2,8,64,256]{3,2,1,0:T(8,128)(2,1)S(1)}, u32[]{:S(2)}, u32[]{:S(2)}) collective-permute-start(bf16[2,8,64,256]{3,2,1,0:T(8,128)(2,1)S(1)} %pad_maximum_fusion.rest_0_), channel_id=1, source_target_pairs={{0,6},{1,25},{2,0},{3,27},{4,2},{5,29},{6,4},{7,31},{8,14},{9,1},{... | collective-permute-start | bytes 1572872 | tf_op jit(solution)/shard_map/ppermute | solution.py:171
  43.4 16.7 %collective-permute-start.8 = (bf16[2,8,64,256]{3,2,1,0:T(8,128)(2,1)S(1)}, bf16[2,8,64,256]{3,2,1,0:T(8,128)(2,1)S(1)}, u32[]{:S(2)}, u32[]{:S(2)}) collective-permute-start(bf16[2,8,64,256]{3,2,1,0:T(8,128)(2,1)S(1)} %constant_dynamic-update-slice_fusion.rest_1_), channel_id=1, source_target_pairs={{0,1},{1,0},{2,3},{3,2},{4,5},{5,4},{6,7},{7,6},{8,9},{9,8},{10,11... | collective-permute-start | bytes 1572872 | tf_op jit(solution)/shard_map/ppermute | solution.py:175
  47.1 13.2 %collective-permute-start.7 = (bf16[2,8,64,256]{3,2,1,0:T(8,128)(2,1)S(1)}, bf16[2,8,64,256]{3,2,1,0:T(8,128)(2,1)S(1)}, u32[]{:S(2)}, u32[]{:S(2)}) collective-permute-start(bf16[2,8,64,256]{3,2,1,0:T(8,128)(2,1)S(1)} %pad_maximum_fusion.rest_0_), channel_id=1, source_target_pairs={{0,1},{1,0},{2,3},{3,2},{4,5},{5,4},{6,7},{7,6},{8,9},{9,8},{10,11... | collective-permute-start | bytes 1572872 | tf_op jit(solution)/shard_map/ppermute | solution.py:175
  47.1 13.4 %collective-permute-start.6 = (bf16[2,8,64,256]{3,2,1,0:T(8,128)(2,1)S(1)}, bf16[2,8,64,256]{3,2,1,0:T(8,128)(2,1)S(1)}, u32[]{:S(2)}, u32[]{:S(2)}) collective-permute-start(bf16[2,8,64,256]{3,2,1,0:T(8,128)(2,1)S(1)} %collective-permute-done.5.rest_3_), channel_id=1, source_target_pairs={{0,6},{1,25},{2,0},{3,27},{4,2},{5,29},{6,4},{7,31},{8,14},{9,1},{... | collective-permute-start | bytes 1572872 | tf_op jit(solution)/shard_map/ppermute | solution.py:171
  56.5 10.5 %collective-permute-start.2 = (bf16[2,8,64,256]{3,2,1,0:T(8,128)(2,1)}, bf16[2,8,64,256]{3,2,1,0:T(8,128)(2,1)S(1)}, u32[]{:S(2)}, u32[]{:S(2)}) collective-permute-start(bf16[2,8,64,256]{3,2,1,0:T(8,128)(2,1)} %collective-permute-done.1.rest_2_), channel_id=1, source_target_pairs={{0,2},{1,9},{2,4},{3,11},{4,6},{5,13},{6,0},{7,15},{8,10},{9,17},{... | collective-permute-start | bytes 1572872 | tf_op jit(solution)/shard_map/ppermute | solution.py:171
  56.6 13.9 %collective-permute-start.13 = (bf16[2,8,64,256]{3,2,1,0:T(8,128)(2,1)}, bf16[2,8,64,256]{3,2,1,0:T(8,128)(2,1)S(1)}, u32[]{:S(2)}, u32[]{:S(2)}) collective-permute-start(bf16[2,8,64,256]{3,2,1,0:T(8,128)(2,1)} %collective-permute-done.1.rest_2_), channel_id=1, source_target_pairs={{0,1},{1,0},{2,3},{3,2},{4,5},{5,4},{6,7},{7,6},{8,9},{9,8},{10,11... | collective-permute-start | bytes 1572872 | tf_op jit(solution)/shard_map/ppermute | solution.py:175
  60.0 10.5 %collective-permute-start.14 = (bf16[2,8,64,256]{3,2,1,0:T(8,128)(2,1)S(1)}, bf16[2,8,64,256]{3,2,1,0:T(8,128)(2,1)S(1)}, u32[]{:S(2)}, u32[]{:S(2)}) collective-permute-start(bf16[2,8,64,256]{3,2,1,0:T(8,128)(2,1)S(1)} %collective-permute-done.5.rest_3_), channel_id=1, source_target_pairs={{0,1},{1,0},{2,3},{3,2},{4,5},{5,4},{6,7},{7,6},{8,9},{9,8},{10,11... | collective-permute-start | bytes 1572872 | tf_op jit(solution)/shard_map/ppermute | solution.py:175
  60.3 10.2 %collective-permute-start.15 = (bf16[2,8,64,256]{3,2,1,0:T(8,128)(2,1)S(1)}, bf16[2,8,64,256]{3,2,1,0:T(8,128)(2,1)S(1)}, u32[]{:S(2)}, u32[]{:S(2)}) collective-permute-start(bf16[2,8,64,256]{3,2,1,0:T(8,128)(2,1)S(1)} %collective-permute-done.9.rest_2_), channel_id=1, source_target_pairs={{0,1},{1,0},{2,3},{3,2},{4,5},{5,4},{6,7},{7,6},{8,9},{9,8},{10,11... | collective-permute-start | bytes 1572872 | tf_op jit(solution)/shard_map/ppermute | solution.py:175
  60.5 10.0 %collective-permute-start.16 = (bf16[2,8,64,256]{3,2,1,0:T(8,128)(2,1)S(1)}, bf16[2,8,64,256]{3,2,1,0:T(8,128)(2,1)S(1)}, u32[]{:S(2)}, u32[]{:S(2)}) collective-permute-start(bf16[2,8,64,256]{3,2,1,0:T(8,128)(2,1)S(1)} %collective-permute-done.10.rest_3_), channel_id=1, source_target_pairs={{0,1},{1,0},{2,3},{3,2},{4,5},{5,4},{6,7},{7,6},{8,9},{9,8},{10,11... | collective-permute-start | bytes 1572872 | tf_op jit(solution)/shard_map/ppermute | solution.py:175
  67.1 9.7 %collective-permute-start.12 = (bf16[2,8,64,256]{3,2,1,0:T(8,128)(2,1)S(1)}, bf16[2,8,64,256]{3,2,1,0:T(8,128)(2,1)S(1)}, u32[]{:S(2)}, u32[]{:S(2)}) collective-permute-start(bf16[2,8,64,256]{3,2,1,0:T(8,128)(2,1)S(1)} %collective-permute-done.6.rest_1_), channel_id=1, source_target_pairs={{0,1},{1,0},{2,3},{3,2},{4,5},{5,4},{6,7},{7,6},{8,9},{9,8},{10,11... | collective-permute-start | bytes 1572872 | tf_op jit(solution)/shard_map/ppermute | solution.py:175
  70.5 6.3 %collective-permute-start.11 = (bf16[2,8,64,256]{3,2,1,0:T(8,128)(2,1)S(1)}, bf16[2,8,64,256]{3,2,1,0:T(8,128)(2,1)S(1)}, u32[]{:S(2)}, u32[]{:S(2)}) collective-permute-start(bf16[2,8,64,256]{3,2,1,0:T(8,128)(2,1)S(1)} %collective-permute-done.2.rest_0_), channel_id=1, source_target_pairs={{0,1},{1,0},{2,3},{3,2},{4,5},{5,4},{6,7},{7,6},{8,9},{9,8},{10,11... | collective-permute-start | bytes 1572872 | tf_op jit(solution)/shard_map/ppermute | solution.py:175
